TPU v7x, 32 devices: a whole 2x2x4 slice. The times are simulated.
32 devices in a mesh: gx: 4 (over y, core), gy: 2 (over x), ta: 4 (over z).
Axes of the slice: x: 2, y: 2, z: 4, core: 2. Of those that a mesh axis runs over, the one named last changes fastest.
Arguments:
- link_x: float32 [2, 3, 3, 16, 16, 256], P(None, None, None, 'gx', 'ta', 'gy'), may hold values from -1 to 1, as said below
- link_t: float32 [2, 3, 3, 16, 16, 256], P(None, None, None, 'gx', 'ta', 'gy'), may hold values from -1 to 1, as said below
Outputs:
- loops: float32 [6, 6, 16, 16], P(None, None, 'gx', 'ta')
Inputs may be any that keep to these rules, and one draw needn't show every extreme that they name: `link_x`: every link matrix is special unitary. `link_t`: every link matrix is special unitary.
All inputs are finite; a program needn't handle non-finite values.
Results may differ from a plain program's by a relative error of at most 0.0001.
Values sent between devices are 32-bit elements; how exact they have to be, the bound alone decides.
No kernel may reach another device: no remote copies, remote signals or barrier semaphores. Data moves between devices by JAX's collectives and lax.ppermute only.
A program may use at most 128 MiB of HBM per device.

v0:
```python
import jax
import jax.numpy as jnp
from jax import lax
from jax.experimental import pallas as pl
from jax.experimental.pallas import tpu as pltpu
from jax.sharding import PartitionSpec as P


RMAX = 6
TMAX = 6


def mul(a, b):
    return a[0] * b[0] - a[1] * b[1], a[0] * b[1] + a[1] * b[0]


def mul_conj(a, b):
    return a[0] * b[0] + a[1] * b[1], a[1] * b[0] - a[0] * b[1]


def add(a, b):
    return a[0] + b[0], a[1] + b[1]


def product(a, b):
    return [
        [add(add(mul(row[0], b[0][k]), mul(row[1], b[1][k])), mul(row[2], b[2][k])) for k in range(3)]
        for row in a
    ]


def product_dagger(a, b):
    return [
        [
            add(add(mul_conj(row[0], b[k][0]), mul_conj(row[1], b[k][1])), mul_conj(row[2], b[k][2]))
            for k in range(3)
        ]
        for row in a
    ]


def completed(a):
    last = []
    for k in range(3):
        i, j = (k + 1) % 3, (k + 2) % 3
        p, q = mul(a[0][i], a[1][j]), mul(a[0][j], a[1][i])
        last.append((p[0] - q[0], q[1] - p[1]))
    return [a[0], a[1], last]


def get(load, rows=2):
    return [[(load((3 * i + j) * 2), load((3 * i + j) * 2 + 1)) for j in range(3)] for i in range(rows)]


def put(store, a):
    for i, row in enumerate(a):
        for j in range(3):
            for k in range(2):
                store((3 * i + j) * 2 + k, row[j][k])


def where(mask, a, b):
    return [[tuple(jnp.where(mask, p, q) for p, q in zip(u, v)) for u, v in zip(r, s)] for r, s in zip(a, b)]


def unit(shape, rows=2):
    one, zero = jnp.ones(shape, jnp.float32), jnp.zeros(shape, jnp.float32)
    return [[(one if i == j else zero, zero) for j in range(3)] for i in range(rows)]


def gauge_kernel(n, links_ref, near_ref, far_ref, edge_ref, g_ref, u_ref):
    lanes = links_ref.shape[-1]
    x_ref, t_ref = links_ref.at[0], links_ref.at[1]

    def raw(ref, t, rows):
        part = lambda p, i, j: ref[p * 9 + i * 3 + j, pl.ds(t, n, stride=n), :]
        return [[(part(0, i, j), part(1, i, j)) for j in range(3)] for i in range(rows)]

    g = unit((n, lanes))
    for t in range(n):
        rows = pl.ds(t * n, n)
        put(lambda c, v: g_ref.__setitem__((c, rows), v), completed(g))
        full = raw(x_ref, t, 3)
        put(lambda c, v: u_ref.__setitem__((c, rows), v), product(g, full) if t else full[:2])
        step = raw(t_ref, t, 3)
        g = product(g, step) if t else step[:2]
    put(lambda c, v: near_ref.__setitem__((c, pl.ds(n * n + n, n)), v), g)
    put(
        lambda c, v: near_ref.__setitem__((c, pl.ds(n * n, n)), v),
        get(lambda c: g_ref[c, pl.ds(0, n, stride=n), :]),
    )
    for i in range(0, n * n, 8):
        last = lax.broadcasted_iota(jnp.int32, (8, lanes), 0) % n == n - 1
        after = where(last, unit((8, lanes), 3), get(lambda c: g_ref[c, pl.ds(i + 1, 8), :], 3))
        w = product_dagger(get(lambda c: u_ref[c, pl.ds(i, 8), :]), after)
        put(lambda c, v: near_ref.__setitem__((c, pl.ds(i, 8)), v), w)
    two = 2 * n
    for c in range(12):
        far_ref[pl.ds(c * (two + 2), two), :] = near_ref[c, pl.ds(0, two), :]
        far_ref[pl.ds(c * (two + 2) + two, 2), :] = near_ref[c, pl.ds(n * n, 2), :]
        edge_ref[pl.ds(c * two, n), :] = near_ref[c, pl.ds(0, n, stride=n), :]
        edge_ref[pl.ds(c * two + n, n), :] = near_ref[c, pl.ds(n * n, n), :]


def chain_kernel(n, own_ref, near_ref, far_ref, out_ref, edge_ref, p_ref):
    lanes = own_ref.shape[-1]
    late, two = n + 2, 2 * n
    size = late * (n + 1)
    store_w = lambda first, count: lambda c, v: out_ref.__setitem__((pl.ds(c * size + first, count),), v)

    def spread(p):
        p = completed(p)
        for k in range(3):
            put(lambda c, v: p_ref.__setitem__((c, pl.ds(k * n, n)), v), p)
        left = get(lambda c: p_ref[c, pl.ds(0, two), :])
        right = get(lambda c: p_ref[c, pl.ds(1, two), :], 3)
        last = lax.broadcasted_iota(jnp.int32, (two, lanes), 0) % n == n - 1
        return left, where(last, unit((two, lanes), 3), right)

    def first_of(p, count):
        return [[tuple(jnp.broadcast_to(e[0:1], (count, lanes)) for e in q) for q in row] for row in p]

    end = pl.ds(n * n + n, n)
    p = get(lambda c: own_ref[c, end, :])
    p_next = get(lambda c: near_ref[c, end, :])
    pp = product(p, completed(p_next))
    left, right = spread(p)
    for i in range(0, n * n, 8):
        w = get(lambda c: near_ref[c, pl.ds(i, 8), :])
        w = product_dagger(product(left, completed(w)), right)
        put(store_w(i, 8), w)
    g = get(lambda c: near_ref[c, pl.ds(n * n, n), :])
    put(store_w(late * n, n), product(first_of(p, n), completed(g)))
    left, right = spread(pp)
    w = get(lambda c: far_ref[pl.ds(c * (two + 2), two), :])
    w = product_dagger(product(left, completed(w)), right)
    put(store_w(n * n, two), w)
    g = get(lambda c: far_ref[pl.ds(c * (two + 2) + two, 2), :])
    put(store_w(late * n + n, 2), product(first_of(pp, 2), completed(g)))
    for c in range(12):
        edge_ref[pl.ds(c * 2 * late, late), :] = out_ref[pl.ds(c * size, late, stride=n), :]
        edge_ref[pl.ds(c * 2 * late + late, late), :] = out_ref[pl.ds(c * size + late * n, late), :]


def loop_kernel(
    n, own_ref, own2_ref, near_ref, near2_ref, far_ref, far2_ref, out_ref, a_ref, b_ref, c_ref, s_ref
):
    lanes = own_ref.shape[-1]
    late, early = n + 2, n * n
    times = n + late
    count = times * n
    size = late * (n + 1)
    pad = 8
    for c in range(12):
        for ref, src, src2 in ((a_ref, own_ref, own2_ref), (b_ref, near_ref, near2_ref)):
            for i in range(0, early, 8):
                ref[c, pl.ds(pad + i, 8), :] = src[c, pl.ds(i, 8), :]
            for i in range(0, late * n, 8):
                ref[c, pl.ds(pad + early + i, 8), :] = src2[pl.ds(c * size + i, 8), :]
        c_ref[c, pl.ds(n - 1, n, stride=n), :] = far_ref[pl.ds(c * 2 * n, n), :]
        c_ref[c, pl.ds(early + n - 1, late, stride=n), :] = far2_ref[pl.ds(c * 2 * late, late), :]
    for ref, g_of in (
        (
            a_ref,
            (
                lambda c: near_ref[c, pl.ds(early, n), :],
                lambda c: near2_ref[pl.ds(c * size + late * n, late), :],
            ),
        ),
        (
            b_ref,
            (
                lambda c: far_ref[pl.ds(c * 2 * n + n, n), :],
                lambda c: far2_ref[pl.ds(c * 2 * late + late, late), :],
            ),
        ),
    ):
        for first, m, g in ((0, n, g_of[0]), (n, late, g_of[1])):
            rows = pl.ds(pad + n - 1 + first * n, m, stride=n)
            v = product_dagger(get(lambda c: ref[c, rows, :]), completed(get(g)))
            put(lambda c, e: ref.__setitem__((c, rows), e), v)

    x_of = lax.broadcasted_iota(jnp.int32, (8, lanes), 0) % n

    def window(k, i):
        if k == 0:
            return get(lambda c: a_ref[c, pl.ds(pad + i, 8), :])
        if k < n:
            return where(
                x_of < n - k,
                get(lambda c: a_ref[c, pl.ds(pad + i + k, 8), :]),
                get(lambda c: b_ref[c, pl.ds(pad + i + k - n, 8), :]),
            )
        if k == n:
            return get(lambda c: b_ref[c, pl.ds(pad + i, 8), :])
        return where(
            x_of < n - 1,
            get(lambda c: b_ref[c, pl.ds(pad + i + 1, 8), :]),
            get(lambda c: c_ref[c, pl.ds(i, 8), :]),
        )

    for i in range(0, count, 8):
        s = window(0, i)
        for r in range(RMAX):
            if r:
                s = product(s, completed(window(r, i)))
            put(lambda c, v: s_ref.__setitem__((r * 18 + c, pl.ds(i, 8)), v), completed(s))

    lane = lax.broadcasted_iota(jnp.int32, (8, lanes), 1)
    packed = [jnp.zeros((8, lanes), jnp.float32)] * 2
    for r in range(RMAX):
        sums = [[None, None] for _ in range(TMAX)]
        for c in range(18):
            at = {t: s_ref[r * 18 + c, pl.ds(t * n, 8), :] for t in range(times - 1)}
            for u in range(1, TMAX + 1):
                for h in range(2):
                    e = at[2 * h] * at[2 * h + u]
                    sums[u - 1][h] = e if c == 0 else sums[u - 1][h] + e
        for u in range(TMAX):
            for h in range(2):
                total = jnp.sum(sums[u][h], axis=1, keepdims=True)
                packed[h] = jnp.where(lane == r * TMAX + u, total, packed[h])
    for h in range(2):
        out_ref[pl.ds(8 * h, 8), :] = packed[h]


def last_kernel(n, scale, own_ref, other_ref, out_ref, v_ref):
    lanes = own_ref.shape[-1]
    total = (own_ref[...] + other_ref[...]) * scale
    for r in range(RMAX):
        v_ref[r] = pltpu.roll(total, lanes - r * TMAX, 1) if r else total
        for x in range(n):
            out_ref[r, x] = v_ref[r, pl.ds(x, n, stride=n), :][:, :TMAX]


def call(kernel, outs, scratch, *args, space=pltpu.VMEM):
    return pl.pallas_call(
        kernel,
        out_shape=[jax.ShapeDtypeStruct(s, jnp.float32) for s in outs],
        in_specs=[pl.BlockSpec(memory_space=space)] * len(args),
        out_specs=[pl.BlockSpec(memory_space=pltpu.VMEM)] * len(outs),
        scratch_shapes=[pltpu.VMEM(s, jnp.float32) if isinstance(s, tuple) else s for s in scratch],
        compiler_params=pltpu.CompilerParams(vmem_limit_bytes=8 * 2**20),
    )(*args)


def ahead(block, axis, distance):
    count = lax.axis_size(axis)
    return lax.ppermute(block, axis, [((i + distance) % count, i) for i in range(count)])


def local(link_x, link_t):
    n, lanes = link_x.shape[3], link_x.shape[5]
    if (n, link_x.shape[4], lanes) != (4, 4, 128):
        return plain(link_x, link_t)
    late = n + 2
    times = n + late
    flat = (18, n * n, lanes)
    own, far, edge = call(
        lambda *refs: gauge_kernel(n, *refs),
        [(12, n * n + 2 * n, lanes), (12 * (2 * n + 2), lanes), (12 * 2 * n, lanes)],
        [(18, n * n + 8, lanes), (12, n * n, lanes)],
        jnp.stack([link_x.reshape(flat), link_t.reshape(flat)]),
    )
    near_t, far_t = ahead(own, "ta", 1), ahead(far, "ta", 2)
    near_x, edge_x = ahead(own, "gx", 1), ahead(edge, "gx", 2)
    own2, edge2 = call(
        lambda *refs: chain_kernel(n, *refs),
        [(12 * late * (n + 1), lanes), (12 * 2 * late, lanes)],
        [(18, 3 * n, lanes)],
        own,
        near_t,
        far_t,
    )
    near2_x, edge2_x = ahead(own2, "gx", 1), ahead(edge2, "gx", 2)
    rows = times * n + 16
    (packed,) = call(
        lambda *refs: loop_kernel(n, *refs),
        [(16, lanes)],
        [(12, rows, lanes), (12, rows, lanes), (12, times * n, lanes), (RMAX * 18, times * n, lanes)],
        own,
        own2,
        near_x,
        near2_x,
        edge_x,
        edge2_x,
    )
    count = lax.axis_size("gy")
    other = ahead(packed, "gy", 1) if count == 2 else lax.psum(packed, "gy") - packed
    scale = 1.0 / (3.0 * (lanes * count))
    (out,) = call(
        lambda *refs: last_kernel(n, scale, *refs),
        [(RMAX, n, n, TMAX)],
        [(RMAX, 4 * n, lanes)],
        packed,
        other,
    )
    return out.transpose(0, 3, 1, 2)


def shifted_2(block, axis, distance):
    devices = range(lax.axis_size(axis))
    route = [((i - distance) % len(devices), i) for i in devices]
    return lax.ppermute(block, axis, route)


def plain_times(left_mat, right_mat):
    real_rows = []
    imag_rows = []
    for i in range(3):
        real_cols = []
        imag_cols = []
        for k in range(3):
            real_sum = (
                left_mat[0, i, 0] * right_mat[0, 0, k] - left_mat[1, i, 0] * right_mat[1, 0, k]
            )
            imag_sum = (
                left_mat[0, i, 0] * right_mat[1, 0, k] + left_mat[1, i, 0] * right_mat[0, 0, k]
            )
            for j in range(1, 3):
                real_sum = (
                    real_sum
                    + left_mat[0, i, j] * right_mat[0, j, k]
                    - left_mat[1, i, j] * right_mat[1, j, k]
                )
                imag_sum = (
                    imag_sum
                    + left_mat[0, i, j] * right_mat[1, j, k]
                    + left_mat[1, i, j] * right_mat[0, j, k]
                )
            real_cols.append(real_sum)
            imag_cols.append(imag_sum)
        real_rows.append(jnp.stack(real_cols))
        imag_rows.append(jnp.stack(imag_cols))
    return jnp.stack([jnp.stack(real_rows), jnp.stack(imag_rows)])


def correlation(upper_half, lower_half):
    return jnp.sum(upper_half * lower_half, axis=(0, 1, 2, 5))


def next_x(field, along_dim):
    edge_cells = shifted_2(lax.slice_in_dim(field, 0, 1, axis=along_dim), "gx", -1)
    inner = lax.slice_in_dim(field, 1, field.shape[along_dim], axis=along_dim)
    return jnp.concatenate([inner, edge_cells], axis=along_dim)


def next_t(field):
    edge_cells = shifted_2(lax.slice_in_dim(field, 0, 1, axis=4), "ta", -1)
    inner = lax.slice_in_dim(field, 1, field.shape[4], axis=4)
    return jnp.concatenate([inner, edge_cells], axis=4)


def plain(link_x, link_t):
    all_rows = []
    temporal = [link_t]
    factor = link_t
    for _ in range(1, TMAX):
        factor = next_t(factor)
        temporal.append(plain_times(temporal[-1], factor))
    carried = jnp.stack(temporal)
    spatial = link_x
    factor_x = link_x
    for radius in range(RMAX):
        if radius > 0:
            factor_x = next_x(factor_x, 3)
            spatial = plain_times(spatial, factor_x)
        carried = next_x(carried, 4)
        shifted = spatial
        row_sums = []
        for extent in range(TMAX):
            shifted = next_t(shifted)
            upper_half = plain_times(spatial, carried[extent])
            lower_half = plain_times(temporal[extent], shifted)
            row_sums.append(correlation(upper_half, lower_half))
        all_rows.append(jnp.stack(row_sums))
    local_sums = jnp.stack(all_rows)
    totals = lax.psum(local_sums, "gy")
    return totals / (3.0 * (link_x.shape[5] * lax.axis_size("gy")))


def solution(mesh):
    return jax.shard_map(
        local,
        mesh=mesh,
        in_specs=(P(None, None, None, "gx", "ta", "gy"), P(None, None, None, "gx", "ta", "gy")),
        out_specs=P(None, None, "gx", "ta"),
        check_vma=False,
    )
```

profile of v0, /device:TPU:0, one launch (start us, length us, event | category | flops | bytes accessed | tf_op | source)
XLA Modules:
  0.0 27.6 jit_solution(4374069208644166806)
XLA Ops:
  0.0 1.0 %pad_maximum_fusion.refs_0_ = f32[2,18,16,128]{3,2,1,0:T(8,128)S(1)} fusion(f32[1,18,16,128]{3,2,1,0:T(8,128)} %bitcast.3, f32[1,18,16,128]{3,2,1,0:T(8,128)} %bitcast.4), kind=kLoop, calls=%fused_computation | loop fusion | flops 73728 | bytes 589824 | tf_op jit(solution)/shard_map/stack | solution.py:263
  1.0 0.2 shard_map.28
  1.2 5.1 %collective-permute-start = (f32[12,24,128]{2,1,0:T(8,128)S(1)}, f32[12,24,128]{2,1,0:T(8,128)S(1)}, u32[]{:S(2)}, u32[]{:S(2)}) collective-permute-start(f32[12,24,128]{2,1,0:T(8,128)S(1)} %get-tuple-element.10.refs_0_), channel_id=1, source_target_pairs={{1,0},{2,1},{3,2},{0,3},{5,4},{6,5},{7,6},{4,7},{9,8},{10,9},{11,1... | collective-permute-start | bytes 442376 | tf_op jit(solution)/shard_map/ppermute | solution.py:249
  6.3 0.0 collective-permute-start.1
  6.3 5.8 %collective-permute-done.1.refs_2_ = f32[120,128]{1,0:T(8,128)S(1)} collective-permute-done((f32[120,128]{1,0:T(8,128)S(1)}, f32[120,128]{1,0:T(8,128)S(1)}, u32[]{:S(2)}, u32[]{:S(2)}) %collective-permute-start.1) | collective-permute-done | bytes 61472 | tf_op jit(solution)/shard_map/ppermute | solution.py:249
  12.1 0.0 collective-permute-done.refs_1_
  12.1 0.2 shard_map.29
  12.4 0.1 collective-permute-start.3
  12.4 1.6 %collective-permute-start.2 = (f32[12,24,128]{2,1,0:T(8,128)S(1)}, f32[12,24,128]{2,1,0:T(8,128)S(1)}, u32[]{:S(2)}, u32[]{:S(2)}) collective-permute-start(f32[12,24,128]{2,1,0:T(8,128)S(1)} %get-tuple-element.10.refs_0_), channel_id=1, source_target_pairs={{8,0},{16,8},{24,16},{0,24},{9,1},{17,9},{25,17},{1,25},{10,2},{18... | collective-permute-start | bytes 442376 | tf_op jit(solution)/shard_map/ppermute | solution.py:249
  14.1 0.5 %collective-permute-start.5 = (f32[144,128]{1,0:T(8,128)S(1)}, f32[144,128]{1,0:T(8,128)S(1)}, u32[]{:S(2)}, u32[]{:S(2)}) collective-permute-start(f32[144,128]{1,0:T(8,128)S(1)} %get-tuple-element.14), channel_id=1, source_target_pairs={{16,0},{24,8},{0,16},{8,24},{17,1},{25,9},{1,17},{9,25},{18,2},{26... | collective-permute-start | bytes 221192 | tf_op jit(solution)/shard_map/ppermute | solution.py:249
  14.6 1.5 %collective-permute-start.4 = (f32[96,128]{1,0:T(8,128)S(1)}, f32[96,128]{1,0:T(8,128)S(1)}, u32[]{:S(2)}, u32[]{:S(2)}) collective-permute-start(f32[96,128]{1,0:T(8,128)S(1)} %get-tuple-element.13), channel_id=1, source_target_pairs={{16,0},{24,8},{0,16},{8,24},{17,1},{25,9},{1,17},{9,25},{18,2},{26... | collective-permute-start | bytes 147464 | tf_op jit(solution)/shard_map/ppermute | solution.py:249
  16.1 5.6 %collective-permute-done.4.refs_4_ = f32[96,128]{1,0:T(8,128)S(1)} collective-permute-done((f32[96,128]{1,0:T(8,128)S(1)}, f32[96,128]{1,0:T(8,128)S(1)}, u32[]{:S(2)}, u32[]{:S(2)}) %collective-permute-start.4) | collective-permute-done | bytes 49184 | tf_op jit(solution)/shard_map/ppermute | solution.py:249
  21.7 0.0 collective-permute-done.2.refs_2_
  21.7 0.0 collective-permute-done.5.refs_5_
  21.7 0.0 collective-permute-done.3.refs_3_
  21.7 1.5 %shard_map.30.refs_0_ = f32[16,128]{1,0:T(8,128)S(1)} custom-call(f32[12,24,128]{2,1,0:T(8,128)S(1)} %get-tuple-element.10.refs_0_, f32[360,128]{1,0:T(8,128)S(1)} %get-tuple-element.12.refs_1_, f32[12,24,128]{2,1,0:T(8,128)S(1)} %collective-permute-done.2.refs_2_, f32[360,128]{1,0:T(8,128)S(1)} %collective-permute-done.3.refs_3_, ...), custom_call_target="tpu_custom_call" | custom-call | tf_op jit(solution)/shard_map/pallas_call | solution.py:237
  23.2 1.5 %collective-permute-start.6 = (f32[16,128]{1,0:T(8,128)S(1)}, f32[16,128]{1,0:T(8,128)S(1)}, u32[]{:S(2)}, u32[]{:S(2)}) collective-permute-start(f32[16,128]{1,0:T(8,128)S(1)} %shard_map.30.refs_0_), channel_id=1, source_target_pairs={{4,0},{0,4},{5,1},{1,5},{6,2},{2,6},{7,3},{3,7},{12,8},{8,12},{13,... | collective-permute-start | bytes 24584 | tf_op jit(solution)/shard_map/ppermute | solution.py:249
  24.7 2.2 %collective-permute-done.6.refs_1_ = f32[16,128]{1,0:T(8,128)S(1)} collective-permute-done((f32[16,128]{1,0:T(8,128)S(1)}, f32[16,128]{1,0:T(8,128)S(1)}, u32[]{:S(2)}, u32[]{:S(2)}) %collective-permute-start.6) | collective-permute-done | bytes 8224 | tf_op jit(solution)/shard_map/ppermute | solution.py:249
  26.9 0.7 %shard_map.31 = f32[6,4,4,6]{3,2,1,0:T(4,128)} custom-call(f32[16,128]{1,0:T(8,128)S(1)} %shard_map.30.refs_0_, f32[16,128]{1,0:T(8,128)S(1)} %collective-permute-done.6.refs_1_), custom_call_target="tpu_custom_call" | custom-call | tf_op jit(solution)/shard_map/pallas_call | solution.py:237
Async XLA Ops:
  1.2 10.9 %collective-permute-start = (f32[12,24,128]{2,1,0:T(8,128)S(1)}, f32[12,24,128]{2,1,0:T(8,128)S(1)}, u32[]{:S(2)}, u32[]{:S(2)}) collective-permute-start(f32[12,24,128]{2,1,0:T(8,128)S(1)} %get-tuple-element.10.refs_0_), channel_id=1, source_target_pairs={{1,0},{2,1},{3,2},{0,3},{5,4},{6,5},{7,6},{4,7},{9,8},{10,9},{11,1... | collective-permute-start | bytes 442376 | tf_op jit(solution)/shard_map/ppermute | solution.py:249
  6.3 5.8 %collective-permute-start.1 = (f32[120,128]{1,0:T(8,128)S(1)}, f32[120,128]{1,0:T(8,128)S(1)}, u32[]{:S(2)}, u32[]{:S(2)}) collective-permute-start(f32[120,128]{1,0:T(8,128)S(1)} %get-tuple-element.11), channel_id=1, source_target_pairs={{2,0},{3,1},{0,2},{1,3},{6,4},{7,5},{4,6},{5,7},{10,8},{11,9},{8,1... | collective-permute-start | bytes 184328 | tf_op jit(solution)/shard_map/ppermute | solution.py:249
  12.4 9.3 %collective-permute-start.3 = (f32[360,128]{1,0:T(8,128)S(1)}, f32[360,128]{1,0:T(8,128)S(1)}, u32[]{:S(2)}, u32[]{:S(2)}) collective-permute-start(f32[360,128]{1,0:T(8,128)S(1)} %get-tuple-element.12.refs_1_), channel_id=1, source_target_pairs={{8,0},{16,8},{24,16},{0,24},{9,1},{17,9},{25,17},{1,25},{10,2},{18... | collective-permute-start | bytes 552968 | tf_op jit(solution)/shard_map/ppermute | solution.py:249
  12.4 9.2 %collective-permute-start.2 = (f32[12,24,128]{2,1,0:T(8,128)S(1)}, f32[12,24,128]{2,1,0:T(8,128)S(1)}, u32[]{:S(2)}, u32[]{:S(2)}) collective-permute-start(f32[12,24,128]{2,1,0:T(8,128)S(1)} %get-tuple-element.10.refs_0_), channel_id=1, source_target_pairs={{8,0},{16,8},{24,16},{0,24},{9,1},{17,9},{25,17},{1,25},{10,2},{18... | collective-permute-start | bytes 442376 | tf_op jit(solution)/shard_map/ppermute | solution.py:249
  14.1 7.6 %collective-permute-start.5 = (f32[144,128]{1,0:T(8,128)S(1)}, f32[144,128]{1,0:T(8,128)S(1)}, u32[]{:S(2)}, u32[]{:S(2)}) collective-permute-start(f32[144,128]{1,0:T(8,128)S(1)} %get-tuple-element.14), channel_id=1, source_target_pairs={{16,0},{24,8},{0,16},{8,24},{17,1},{25,9},{1,17},{9,25},{18,2},{26... | collective-permute-start | bytes 221192 | tf_op jit(solution)/shard_map/ppermute | solution.py:249
  14.6 7.1 %collective-permute-start.4 = (f32[96,128]{1,0:T(8,128)S(1)}, f32[96,128]{1,0:T(8,128)S(1)}, u32[]{:S(2)}, u32[]{:S(2)}) collective-permute-start(f32[96,128]{1,0:T(8,128)S(1)} %get-tuple-element.13), channel_id=1, source_target_pairs={{16,0},{24,8},{0,16},{8,24},{17,1},{25,9},{1,17},{9,25},{18,2},{26... | collective-permute-start | bytes 147464 | tf_op jit(solution)/shard_map/ppermute | solution.py:249
  23.2 3.7 %collective-permute-start.6 = (f32[16,128]{1,0:T(8,128)S(1)}, f32[16,128]{1,0:T(8,128)S(1)}, u32[]{:S(2)}, u32[]{:S(2)}) collective-permute-start(f32[16,128]{1,0:T(8,128)S(1)} %shard_map.30.refs_0_), channel_id=1, source_target_pairs={{4,0},{0,4},{5,1},{1,5},{6,2},{2,6},{7,3},{3,7},{12,8},{8,12},{13,... | collective-permute-start | bytes 24584 | tf_op jit(solution)/shard_map/ppermute | solution.py:249
where the time goes:
time: 27.7 us; the launch traced here: 27.6 us
  waiting for transfers between devices  13.5 us (49%)
  starting transfers between devices  10.4 us (38%)
  Pallas kernels  2.67 us (10%)
  other arithmetic  1 us (4%)
    ppermute x7, waiting for transfers between devices, ahead(): lax.ppermute(block, axis, [((i + distance) % count, i) for i in range(cou...  13.5 us
    ppermute x7, starting transfers between devices, ahead(): lax.ppermute(block, axis, [((i + distance) % count, i) for i in range(cou...  10.4 us
    pallas_call x4, Pallas kernels, call(): pl.pallas_call(kernel, out_shape=[jax.ShapeDtypeStruct(s, jnp.float32) fo...  2.67 us
    another operation x1, other arithmetic, local(): jnp.stack([link_x.reshape(flat), link_t.reshape(flat)])  1 us
  transfers between devices with their start and end apart: 7, of which 3 were waited for; matrix products, arithmetic and copies ran while one was open for 0% of the time, Pallas kernels for 0%

commit v1 on v0

v1 whole, which is shorter than its diff:
```python
import jax
import jax.numpy as jnp
from jax import lax
from jax.experimental import pallas as pl
from jax.experimental.pallas import tpu as pltpu
from jax.sharding import PartitionSpec as P


RMAX = 6
TMAX = 6


def mul(a, b):
    return a[0] * b[0] - a[1] * b[1], a[0] * b[1] + a[1] * b[0]


def mul_conj(a, b):
    return a[0] * b[0] + a[1] * b[1], a[1] * b[0] - a[0] * b[1]


def add(a, b):
    return a[0] + b[0], a[1] + b[1]


def product(a, b):
    return [
        [add(add(mul(row[0], b[0][k]), mul(row[1], b[1][k])), mul(row[2], b[2][k])) for k in range(3)]
        for row in a
    ]


def product_dagger(a, b):
    return [
        [
            add(add(mul_conj(row[0], b[k][0]), mul_conj(row[1], b[k][1])), mul_conj(row[2], b[k][2]))
            for k in range(3)
        ]
        for row in a
    ]


def completed(a):
    last = []
    for k in range(3):
        i, j = (k + 1) % 3, (k + 2) % 3
        p, q = mul(a[0][i], a[1][j]), mul(a[0][j], a[1][i])
        last.append((p[0] - q[0], q[1] - p[1]))
    return [a[0], a[1], last]


def get(load, rows=2):
    return [[(load((3 * i + j) * 2), load((3 * i + j) * 2 + 1)) for j in range(3)] for i in range(rows)]


def put(store, a):
    for i, row in enumerate(a):
        for j in range(3):
            for k in range(2):
                store((3 * i + j) * 2 + k, row[j][k])


def where(mask, a, b):
    return [[tuple(jnp.where(mask, p, q) for p, q in zip(u, v)) for u, v in zip(r, s)] for r, s in zip(a, b)]


def unit(shape, rows=2):
    one, zero = jnp.ones(shape, jnp.float32), jnp.zeros(shape, jnp.float32)
    return [[(one if i == j else zero, zero) for j in range(3)] for i in range(rows)]


def pivots(a):
    size = [v[0] * v[0] + v[1] * v[1] for v in a]
    first = jnp.logical_and(size[0] >= size[1], size[0] >= size[2])
    last = jnp.logical_and(jnp.logical_not(first), size[2] > size[1])
    return size, first, last


def pick(mask, p, q):
    return tuple(jnp.where(mask, u, v) for u, v in zip(p, q))


def sent(m):
    a, b = m[0], m[1]
    _, first, last = pivots(a)
    return [e for v in (*a, pick(first, b[1], b[0]), pick(last, b[1], b[2])) for e in v]


def received(load):
    v = [(load(2 * k), load(2 * k + 1)) for k in range(5)]
    a, e, f = v[:3], v[3], v[4]
    size, first, last = pivots(a)
    p, q = pick(first, a[1], a[0]), pick(last, a[1], a[2])
    top = pick(first, a[0], pick(last, a[2], a[1]))
    scale = -1.0 / jnp.maximum(jnp.maximum(size[0], size[1]), size[2])
    g = mul(add(mul_conj(e, p), mul_conj(f, q)), top)
    g = (g[0] * scale, g[1] * scale)
    return [a, [pick(first, g, e), pick(first, e, pick(last, f, g)), pick(last, g, f)]]


def send(store, m):
    for k, e in enumerate(sent(m)):
        store(k, e)


def at_rows(ref, rows_of_value):
    def store(k, v):
        ref[rows_of_value(k)] = v

    return store


def flat_rows(ref, size, first, count, stride=None):
    rows = lambda k: pl.ds(k * size + first, count, stride=stride)
    return lambda k: ref[rows(k), :], at_rows(ref, rows)


def rows_of(ref, first, count, stride=None, offset=0):
    rows = pl.ds(first, count, stride=stride)
    return lambda k: ref[offset + k, rows, :], at_rows(ref, lambda k: (offset + k, rows))


def gauge_kernel(n, links_ref, own_ref, near_ref, far_ref, edge_ref, g_ref, u_ref):
    lanes = links_ref.shape[-1]
    block = n * n
    near, far, edge = block + 2 * n - 1, 2 * n + 1, 2 * n - 1

    def raw(field, t, rows):
        part = lambda p, i, j: links_ref[field, p * 9 + i * 3 + j, pl.ds(t, n, stride=n), :]
        return [[(part(0, i, j), part(1, i, j)) for j in range(3)] for i in range(rows)]

    g = unit((n, lanes))
    for t in range(n):
        put(rows_of(g_ref, t * n, n)[1], completed(g))
        full = raw(0, t, 3)
        put(rows_of(u_ref, t * n, n)[1], product(g, full) if t else full[:2])
        step = raw(1, t, 3)
        g = product(g, step) if t else step[:2]
    put(rows_of(own_ref, block + n, n)[1], g)
    send(flat_rows(near_ref, near, block, n)[1], g)
    g = get(rows_of(g_ref, 0, n, n)[0])
    put(rows_of(own_ref, block, n)[1], g)
    g = [[tuple(e[1:] for e in v) for v in row] for row in g]
    send(flat_rows(near_ref, near, block + n, n - 1)[1], g)
    last = lax.broadcasted_iota(jnp.int32, (8, lanes), 0) % n == n - 1
    for i in range(0, block, 8):
        after = where(last, unit((8, lanes), 3), get(rows_of(g_ref, i + 1, 8)[0], 3))
        w = product_dagger(get(rows_of(u_ref, i, 8)[0]), after)
        put(rows_of(own_ref, i, 8)[1], w)
        send(flat_rows(near_ref, near, i, 8)[1], w)
    for k in range(10):
        far_ref[pl.ds(k * far, 2 * n), :] = near_ref[pl.ds(k * near, 2 * n), :]
        far_ref[pl.ds(k * far + 2 * n, 1), :] = near_ref[pl.ds(k * near + block + n, 1), :]
        edge_ref[pl.ds(k * edge, n), :] = near_ref[pl.ds(k * near, n, stride=n), :]
        edge_ref[pl.ds(k * edge + n, n - 1), :] = near_ref[pl.ds(k * near + block + n, n - 1), :]


def chain_kernel(n, own_ref, near_ref, far_ref, out_ref, late_ref, edge_ref, p_ref):
    lanes = own_ref.shape[-1]
    late, two, block = n + 2, 2 * n, n * n
    size = late * (n + 1)
    near, far = block + 2 * n - 1, 2 * n + 1

    def keep(first, count, m):
        put(flat_rows(out_ref, size, first, count)[1], m)
        send(flat_rows(late_ref, size, first, count)[1], m)

    def spread(p):
        p = completed(p)
        for k in range(3):
            put(rows_of(p_ref, k * n, n)[1], p)
        last = lax.broadcasted_iota(jnp.int32, (two, lanes), 0) % n == n - 1
        right = where(last, unit((two, lanes), 3), get(rows_of(p_ref, 1, two)[0], 3))
        return get(rows_of(p_ref, 0, two)[0]), right

    def first_of(p, count):
        return [[tuple(jnp.broadcast_to(e[0:1], (count, lanes)) for e in q) for q in row] for row in p]

    p = get(rows_of(own_ref, block + n, n)[0])
    p_next = received(flat_rows(near_ref, near, block, n)[0])
    pp = product(p, completed(p_next))
    left, right = spread(p)
    for i in range(0, block, 8):
        w = received(flat_rows(near_ref, near, i, 8)[0])
        keep(i, 8, product_dagger(product(left, completed(w)), right))
    keep(late * n, 1, first_of(p, 1))
    g = received(flat_rows(near_ref, near, block + n, n - 1)[0])
    keep(late * n + 1, n - 1, product(first_of(p, n - 1), completed(g)))
    left, right = spread(pp)
    w = received(flat_rows(far_ref, far, 0, two)[0])
    keep(block, two, product_dagger(product(left, completed(w)), right))
    keep(late * n + n, 1, first_of(pp, 1))
    g = received(flat_rows(far_ref, far, two, 1)[0])
    keep(late * n + n + 1, 1, product(first_of(pp, 1), completed(g)))
    for k in range(10):
        edge_ref[pl.ds(k * 2 * late, late), :] = late_ref[pl.ds(k * size, late, stride=n), :]
        edge_ref[pl.ds(k * 2 * late + late, late), :] = late_ref[pl.ds(k * size + late * n, late), :]


PAD = 8


def transports(n, times, a_ref, b_ref, c_ref, closing, store):
    lanes = a_ref.shape[-1]
    for ref, g in zip((a_ref, b_ref), closing):
        load, keep = rows_of(ref, PAD + n - 1, times, n)
        put(keep, product_dagger(get(load), completed(g)))
    x_of = lax.broadcasted_iota(jnp.int32, (8, lanes), 0) % n

    def window(k, i):
        own = lambda shift: get(rows_of(a_ref, PAD + i + shift, 8)[0])
        after = lambda shift: get(rows_of(b_ref, PAD + i + shift, 8)[0])
        if k == 0:
            return own(0)
        if k < n:
            return where(x_of < n - k, own(k), after(k - n))
        if k == n:
            return after(0)
        return where(x_of < n - 1, after(1), get(rows_of(c_ref, i, 8)[0]))

    for i in range(0, times * n, 8):
        s = window(0, i)
        for r in range(RMAX):
            if r:
                s = product(s, completed(window(r, i)))
            put(lambda c, v: store(r * 18 + c, i, v), completed(s))


def paired(pairs, at):
    sums = [None] * len(pairs)
    for c in range(18):
        for k, (p, q) in enumerate(pairs):
            e = at(c, p) * at(c, q)
            sums[k] = e if c == 0 else sums[k] + e
    return [jnp.sum(v, axis=1, keepdims=True) for v in sums]


def early_kernel(n, own_ref, near_ref, far_ref, s_ref, out_ref, a_ref, b_ref, c_ref, g_ref):
    lanes = own_ref.shape[-1]
    block = n * n
    near, edge = block + 2 * n - 1, 2 * n - 1
    for i in range(0, block, 8):
        put(rows_of(a_ref, PAD + i, 8)[1], get(rows_of(own_ref, i, 8)[0]))
        put(rows_of(b_ref, PAD + i, 8)[1], received(flat_rows(near_ref, near, i, 8)[0]))
    put(rows_of(c_ref, n - 1, n, n)[1], received(flat_rows(far_ref, edge, 0, n)[0]))
    closing = []
    for k, load in enumerate((flat_rows(near_ref, near, block + n, n - 1), flat_rows(far_ref, edge, n, n - 1))):
        put(rows_of(g_ref, 0, 1, offset=12 * k)[1], unit((1, lanes)))
        put(rows_of(g_ref, 1, n - 1, offset=12 * k)[1], received(load[0]))
        closing.append(get(rows_of(g_ref, 0, n, offset=12 * k)[0]))

    def store(c, i, v):
        s_ref[c, pl.ds(i, 8), :] = v

    transports(n, n, a_ref, b_ref, c_ref, closing, store)
    lane = lax.broadcasted_iota(jnp.int32, (8, lanes), 1)
    packed = jnp.zeros((8, lanes), jnp.float32)
    for r in range(RMAX):
        at = lambda c, t: s_ref[r * 18 + c, pl.ds(t * n, 8), :]
        for u, total in enumerate(paired([(0, 1), (0, 2)], at)):
            packed = jnp.where(lane == r * TMAX + u, total, packed)
    out_ref[...] = packed


def late_kernel(n, own_ref, near_ref, far_ref, early_ref, packed_ref, out_ref, a_ref, b_ref, c_ref, s_ref):
    lanes = own_ref.shape[-1]
    late = n + 2
    size = late * (n + 1)
    for i in range(0, late * n, 8):
        put(rows_of(a_ref, PAD + i, 8)[1], get(flat_rows(own_ref, size, i, 8)[0]))
        put(rows_of(b_ref, PAD + i, 8)[1], received(flat_rows(near_ref, size, i, 8)[0]))
    put(rows_of(c_ref, n - 1, late, n)[1], received(flat_rows(far_ref, 2 * late, 0, late)[0]))
    closing = [
        received(flat_rows(near_ref, size, late * n, late)[0]),
        received(flat_rows(far_ref, 2 * late, late, late)[0]),
    ]

    def store(c, i, v):
        s_ref[c, pl.ds(n + i, 8), :] = v

    transports(n, late, a_ref, b_ref, c_ref, closing, store)
    for c in range(RMAX * 18):
        s_ref[c, pl.ds(0, n), :] = early_ref[c, pl.ds(n * n - n, n), :]
    lane = lax.broadcasted_iota(jnp.int32, (8, lanes), 1)
    packed = [packed_ref[...], jnp.zeros((8, lanes), jnp.float32)]
    places = [(h, u) for u in range(1, TMAX + 1) for h in range(2) if (h, u) not in ((0, 1), (0, 2))]
    for r in range(RMAX):

        def at(c, t):
            if t < n - 1:
                return early_ref[r * 18 + c, pl.ds(t * n, 8), :]
            return s_ref[r * 18 + c, pl.ds((t - n + 1) * n, 8), :]

        for (h, u), total in zip(places, paired([(2 * h, 2 * h + u) for h, u in places], at)):
            packed[h] = jnp.where(lane == r * TMAX + u - 1, total, packed[h])
    for h in range(2):
        out_ref[pl.ds(8 * h, 8), :] = packed[h]


def last_kernel(n, scale, own_ref, other_ref, out_ref, v_ref):
    lanes = own_ref.shape[-1]
    total = (own_ref[...] + other_ref[...]) * scale
    for r in range(RMAX):
        v_ref[r] = pltpu.roll(total, lanes - r * TMAX, 1) if r else total
        for x in range(n):
            out_ref[r, x] = v_ref[r, pl.ds(x, n, stride=n), :][:, :TMAX]


def call(kernel, outs, scratch, *args, space=pltpu.VMEM):
    return pl.pallas_call(
        kernel,
        out_shape=[jax.ShapeDtypeStruct(s, jnp.float32) for s in outs],
        in_specs=[pl.BlockSpec(memory_space=space)] * len(args),
        out_specs=[pl.BlockSpec(memory_space=pltpu.VMEM)] * len(outs),
        scratch_shapes=[pltpu.VMEM(s, jnp.float32) if isinstance(s, tuple) else s for s in scratch],
        compiler_params=pltpu.CompilerParams(vmem_limit_bytes=8 * 2**20),
    )(*args)


def ahead(block, axis, distance):
    count = lax.axis_size(axis)
    return lax.ppermute(block, axis, [((i + distance) % count, i) for i in range(count)])


def local(link_x, link_t):
    n, lanes = link_x.shape[3], link_x.shape[5]
    if (n, link_x.shape[4], lanes) != (4, 4, 128):
        return plain(link_x, link_t)
    late, block = n + 2, n * n
    size, two = late * (n + 1), 2 * n
    flat = (18, block, lanes)
    own, near, far, edge = call(
        lambda *refs: gauge_kernel(n, *refs),
        [(12, block + two, lanes)] + [(10 * rows, lanes) for rows in (block + two - 1, two + 1, two - 1)],
        [(18, block + 8, lanes), (12, block, lanes)],
        jnp.stack([link_x.reshape(flat), link_t.reshape(flat)]),
    )
    near_t, far_t = ahead(near, "ta", 1), ahead(far, "ta", 2)
    near_x, edge_x = ahead(near, "gx", 1), ahead(edge, "gx", 2)
    own2, near2, edge2 = call(
        lambda *refs: chain_kernel(n, *refs),
        [(12 * size, lanes), (10 * size, lanes), (10 * 2 * late, lanes)],
        [(18, 3 * n, lanes)],
        own,
        near_t,
        far_t,
    )
    near2_x, edge2_x = ahead(near2, "gx", 1), ahead(edge2, "gx", 2)
    transport = (RMAX * 18, block, lanes)
    spaces = lambda rows: [(12, rows + 2 * PAD, lanes), (12, rows + 2 * PAD, lanes), (12, rows, lanes)]
    early, packed = call(
        lambda *refs: early_kernel(n, *refs),
        [transport, (8, lanes)],
        [*spaces(block), (24, 8, lanes)],
        own,
        near_x,
        edge_x,
    )
    (packed,) = call(
        lambda *refs: late_kernel(n, *refs),
        [(16, lanes)],
        [*spaces(late * n), (RMAX * 18, (late + 1) * n, lanes)],
        own2,
        near2_x,
        edge2_x,
        early,
        packed,
    )
    count = lax.axis_size("gy")
    other = ahead(packed, "gy", 1) if count == 2 else lax.psum(packed, "gy") - packed
    scale = 1.0 / (3.0 * (lanes * count))
    (out,) = call(
        lambda *refs: last_kernel(n, scale, *refs),
        [(RMAX, n, n, TMAX)],
        [(RMAX, 4 * n, lanes)],
        packed,
        other,
    )
    return out.transpose(0, 3, 1, 2)


def shifted_2(block, axis, distance):
    devices = range(lax.axis_size(axis))
    route = [((i - distance) % len(devices), i) for i in devices]
    return lax.ppermute(block, axis, route)


def plain_times(left_mat, right_mat):
    real_rows = []
    imag_rows = []
    for i in range(3):
        real_cols = []
        imag_cols = []
        for k in range(3):
            real_sum = (
                left_mat[0, i, 0] * right_mat[0, 0, k] - left_mat[1, i, 0] * right_mat[1, 0, k]
            )
            imag_sum = (
                left_mat[0, i, 0] * right_mat[1, 0, k] + left_mat[1, i, 0] * right_mat[0, 0, k]
            )
            for j in range(1, 3):
                real_sum = (
                    real_sum
                    + left_mat[0, i, j] * right_mat[0, j, k]
                    - left_mat[1, i, j] * right_mat[1, j, k]
                )
                imag_sum = (
                    imag_sum
                    + left_mat[0, i, j] * right_mat[1, j, k]
                    + left_mat[1, i, j] * right_mat[0, j, k]
                )
            real_cols.append(real_sum)
            imag_cols.append(imag_sum)
        real_rows.append(jnp.stack(real_cols))
        imag_rows.append(jnp.stack(imag_cols))
    return jnp.stack([jnp.stack(real_rows), jnp.stack(imag_rows)])


def correlation(upper_half, lower_half):
    return jnp.sum(upper_half * lower_half, axis=(0, 1, 2, 5))


def next_x(field, along_dim):
    edge_cells = shifted_2(lax.slice_in_dim(field, 0, 1, axis=along_dim), "gx", -1)
    inner = lax.slice_in_dim(field, 1, field.shape[along_dim], axis=along_dim)
    return jnp.concatenate([inner, edge_cells], axis=along_dim)


def next_t(field):
    edge_cells = shifted_2(lax.slice_in_dim(field, 0, 1, axis=4), "ta", -1)
    inner = lax.slice_in_dim(field, 1, field.shape[4], axis=4)
    return jnp.concatenate([inner, edge_cells], axis=4)


def plain(link_x, link_t):
    all_rows = []
    temporal = [link_t]
    factor = link_t
    for _ in range(1, TMAX):
        factor = next_t(factor)
        temporal.append(plain_times(temporal[-1], factor))
    carried = jnp.stack(temporal)
    spatial = link_x
    factor_x = link_x
    for radius in range(RMAX):
        if radius > 0:
            factor_x = next_x(factor_x, 3)
            spatial = plain_times(spatial, factor_x)
        carried = next_x(carried, 4)
        shifted = spatial
        row_sums = []
        for extent in range(TMAX):
            shifted = next_t(shifted)
            upper_half = plain_times(spatial, carried[extent])
            lower_half = plain_times(temporal[extent], shifted)
            row_sums.append(correlation(upper_half, lower_half))
        all_rows.append(jnp.stack(row_sums))
    local_sums = jnp.stack(all_rows)
    totals = lax.psum(local_sums, "gy")
    return totals / (3.0 * (link_x.shape[5] * lax.axis_size("gy")))


def solution(mesh):
    return jax.shard_map(
        local,
        mesh=mesh,
        in_specs=(P(None, None, None, "gx", "ta", "gy"), P(None, None, None, "gx", "ta", "gy")),
        out_specs=P(None, None, "gx", "ta"),
        check_vma=False,
    )
```

time: 27.7 us -> 26.2 us (0.946)
  waiting for transfers between devices: 13.5 us -> 11.6 us
  Pallas kernels: 2.67 us -> 3.08 us
    ppermute x7, waiting for transfers between devices: 13.5 us -> 11.6 us  [ahead(): lax.ppermute(block, axis, [((i + distance) % count, i) for i in range(cou...]
    pallas_call x4 -> x5, Pallas kernels: 2.67 us -> 3.08 us  [call(): pl.pallas_call(kernel, out_shape=[jax.ShapeDtypeStruct(s, jnp.float32) fo...]
  transfers between devices with their start and end apart: 7 -> 7, of which waited for: 3 -> 3; matrix products, arithmetic and copies ran while one was open for 0% -> 0% of each run, Pallas kernels for 0% -> 2%
where the time goes in v1:
time: 26.2 us; the launch traced here: 26.1 us
  waiting for transfers between devices  11.6 us (44%)
  starting transfers between devices  10.4 us (40%)
  Pallas kernels  3.08 us (12%)
  other arithmetic  1 us (4%)
    ppermute x7, waiting for transfers between devices, ahead(): lax.ppermute(block, axis, [((i + distance) % count, i) for i in range(cou...  11.6 us
    ppermute x7, starting transfers between devices, ahead(): lax.ppermute(block, axis, [((i + distance) % count, i) for i in range(cou...  10.4 us
    pallas_call x5, Pallas kernels, call(): pl.pallas_call(kernel, out_shape=[jax.ShapeDtypeStruct(s, jnp.float32) fo...  3.08 us
    another operation x1, other arithmetic, local(): jnp.stack([link_x.reshape(flat), link_t.reshape(flat)])  1 us
  transfers between devices with their start and end apart: 7, of which 3 were waited for; matrix products, arithmetic and copies ran while one was open for 0% of the time, Pallas kernels for 2%

profile of v1, /device:TPU:0, one launch (start us, length us, event | category | flops | bytes accessed | tf_op | source)
XLA Modules:
  0.0 26.1 jit_solution(1370028142936800814)
XLA Ops:
  0.0 1.0 %pad_maximum_fusion.refs_0_ = f32[2,18,16,128]{3,2,1,0:T(8,128)S(1)} fusion(f32[1,18,16,128]{3,2,1,0:T(8,128)} %bitcast.3, f32[1,18,16,128]{3,2,1,0:T(8,128)} %bitcast.4), kind=kLoop, calls=%fused_computation | loop fusion | flops 73728 | bytes 589824 | tf_op jit(solution)/shard_map/stack | solution.py:335
  1.0 0.2 shard_map.28
  1.2 5.1 %collective-permute-start = (f32[230,128]{1,0:T(8,128)S(1)}, f32[230,128]{1,0:T(8,128)S(1)}, u32[]{:S(2)}, u32[]{:S(2)}) collective-permute-start(f32[230,128]{1,0:T(8,128)S(1)} %get-tuple-element.15), channel_id=1, source_target_pairs={{1,0},{2,1},{3,2},{0,3},{5,4},{6,5},{7,6},{4,7},{9,8},{10,9},{11,1... | collective-permute-start | bytes 353288 | tf_op jit(solution)/shard_map/ppermute | solution.py:321
  6.3 0.0 collective-permute-start.1
  6.4 5.0 %collective-permute-done.1.refs_2_ = f32[90,128]{1,0:T(8,128)S(1)} collective-permute-done((f32[90,128]{1,0:T(8,128)S(1)}, f32[90,128]{1,0:T(8,128)S(1)}, u32[]{:S(2)}, u32[]{:S(2)}) %collective-permute-start.1) | collective-permute-done | bytes 46112 | tf_op jit(solution)/shard_map/ppermute | solution.py:321
  11.3 0.0 collective-permute-done.refs_1_
  11.3 0.3 %shard_map.29 = (f32[360,128]{1,0:T(8,128)S(1)}, f32[300,128]{1,0:T(8,128)S(1)}, f32[120,128]{1,0:T(8,128)S(1)}) custom-call(f32[12,24,128]{2,1,0:T(8,128)S(1)} %get-tuple-element.14.refs_0_, f32[230,128]{1,0:T(8,128)S(1)} %collective-permute-done.refs_1_, f32[90,128]{1,0:T(8,128)S(1)} %collective-permute-done.1.refs_2_), custom_call_target="tpu_custom_call" | custom-call | tf_op jit(solution)/shard_map/pallas_call | solution.py:309
  11.7 0.1 collective-permute-start.2
  11.7 1.6 %collective-permute-start.4 = (f32[230,128]{1,0:T(8,128)S(1)}, f32[230,128]{1,0:T(8,128)S(1)}, u32[]{:S(2)}, u32[]{:S(2)}) collective-permute-start(f32[230,128]{1,0:T(8,128)S(1)} %get-tuple-element.15), channel_id=1, source_target_pairs={{8,0},{16,8},{24,16},{0,24},{9,1},{17,9},{25,17},{1,25},{10,2},{18... | collective-permute-start | bytes 353288 | tf_op jit(solution)/shard_map/ppermute | solution.py:321
  13.3 0.5 %collective-permute-start.3 = (f32[120,128]{1,0:T(8,128)S(1)}, f32[120,128]{1,0:T(8,128)S(1)}, u32[]{:S(2)}, u32[]{:S(2)}) collective-permute-start(f32[120,128]{1,0:T(8,128)S(1)} %get-tuple-element.19), channel_id=1, source_target_pairs={{16,0},{24,8},{0,16},{8,24},{17,1},{25,9},{1,17},{9,25},{18,2},{26... | collective-permute-start | bytes 184328 | tf_op jit(solution)/shard_map/ppermute | solution.py:321
  13.9 1.5 %collective-permute-start.5 = (f32[70,128]{1,0:T(8,128)S(1)}, f32[70,128]{1,0:T(8,128)S(1)}, u32[]{:S(2)}, u32[]{:S(2)}) collective-permute-start(f32[70,128]{1,0:T(8,128)S(1)} %get-tuple-element.20), channel_id=1, source_target_pairs={{16,0},{24,8},{0,16},{8,24},{17,1},{25,9},{1,17},{9,25},{18,2},{26... | collective-permute-start | bytes 107528 | tf_op jit(solution)/shard_map/ppermute | solution.py:321
  15.4 4.4 %collective-permute-done.5.refs_2_ = f32[70,128]{1,0:T(8,128)S(1)} collective-permute-done((f32[70,128]{1,0:T(8,128)S(1)}, f32[70,128]{1,0:T(8,128)S(1)}, u32[]{:S(2)}, u32[]{:S(2)}) %collective-permute-start.5) | collective-permute-done | bytes 35872 | tf_op jit(solution)/shard_map/ppermute | solution.py:321
  19.8 0.0 collective-permute-done.4.refs_1_
  19.8 0.6 %shard_map.30 = (f32[108,16,128]{2,1,0:T(8,128)S(1)}, f32[8,128]{1,0:T(8,128)S(1)}) custom-call(f32[12,24,128]{2,1,0:T(8,128)S(1)} %get-tuple-element.14.refs_0_, f32[230,128]{1,0:T(8,128)S(1)} %collective-permute-done.4.refs_1_, f32[70,128]{1,0:T(8,128)S(1)} %collective-permute-done.5.refs_2_), custom_call_target="tpu_custom_call" | custom-call | tf_op jit(solution)/shard_map/pallas_call | solution.py:309
  20.5 0.0 collective-permute-done.3.refs_2_
  20.5 0.0 collective-permute-done.2.refs_1_
  20.5 1.2 %shard_map.31.refs_0_ = f32[16,128]{1,0:T(8,128)S(1)} custom-call(f32[360,128]{1,0:T(8,128)S(1)} %get-tuple-element.17.refs_0_, f32[300,128]{1,0:T(8,128)S(1)} %collective-permute-done.2.refs_1_, f32[120,128]{1,0:T(8,128)S(1)} %collective-permute-done.3.refs_2_, f32[108,16,128]{2,1,0:T(8,128)S(1)} %get-tuple-element.21.refs_3_, ...), custom_call_target="tpu_custom_call" | custom-call | tf_op jit(solution)/shard_map/pallas_call | solution.py:309
  21.7 1.5 %collective-permute-start.6 = (f32[16,128]{1,0:T(8,128)S(1)}, f32[16,128]{1,0:T(8,128)S(1)}, u32[]{:S(2)}, u32[]{:S(2)}) collective-permute-start(f32[16,128]{1,0:T(8,128)S(1)} %shard_map.31.refs_0_), channel_id=1, source_target_pairs={{4,0},{0,4},{5,1},{1,5},{6,2},{2,6},{7,3},{3,7},{12,8},{8,12},{13,... | collective-permute-start | bytes 24584 | tf_op jit(solution)/shard_map/ppermute | solution.py:321
  23.2 2.2 %collective-permute-done.6.refs_1_ = f32[16,128]{1,0:T(8,128)S(1)} collective-permute-done((f32[16,128]{1,0:T(8,128)S(1)}, f32[16,128]{1,0:T(8,128)S(1)}, u32[]{:S(2)}, u32[]{:S(2)}) %collective-permute-start.6) | collective-permute-done | bytes 8224 | tf_op jit(solution)/shard_map/ppermute | solution.py:321
  25.4 0.7 %shard_map.32 = f32[6,4,4,6]{3,2,1,0:T(4,128)} custom-call(f32[16,128]{1,0:T(8,128)S(1)} %shard_map.31.refs_0_, f32[16,128]{1,0:T(8,128)S(1)} %collective-permute-done.6.refs_1_), custom_call_target="tpu_custom_call" | custom-call | tf_op jit(solution)/shard_map/pallas_call | solution.py:309
Async XLA Ops:
  1.2 10.1 %collective-permute-start = (f32[230,128]{1,0:T(8,128)S(1)}, f32[230,128]{1,0:T(8,128)S(1)}, u32[]{:S(2)}, u32[]{:S(2)}) collective-permute-start(f32[230,128]{1,0:T(8,128)S(1)} %get-tuple-element.15), channel_id=1, source_target_pairs={{1,0},{2,1},{3,2},{0,3},{5,4},{6,5},{7,6},{4,7},{9,8},{10,9},{11,1... | collective-permute-start | bytes 353288 | tf_op jit(solution)/shard_map/ppermute | solution.py:321
  6.3 5.0 %collective-permute-start.1 = (f32[90,128]{1,0:T(8,128)S(1)}, f32[90,128]{1,0:T(8,128)S(1)}, u32[]{:S(2)}, u32[]{:S(2)}) collective-permute-start(f32[90,128]{1,0:T(8,128)S(1)} %get-tuple-element.16), channel_id=1, source_target_pairs={{2,0},{3,1},{0,2},{1,3},{6,4},{7,5},{4,6},{5,7},{10,8},{11,9},{8,1... | collective-permute-start | bytes 138248 | tf_op jit(solution)/shard_map/ppermute | solution.py:321
  11.7 8.8 %collective-permute-start.2 = (f32[300,128]{1,0:T(8,128)S(1)}, f32[300,128]{1,0:T(8,128)S(1)}, u32[]{:S(2)}, u32[]{:S(2)}) collective-permute-start(f32[300,128]{1,0:T(8,128)S(1)} %get-tuple-element.18), channel_id=1, source_target_pairs={{8,0},{16,8},{24,16},{0,24},{9,1},{17,9},{25,17},{1,25},{10,2},{18... | collective-permute-start | bytes 460808 | tf_op jit(solution)/shard_map/ppermute | solution.py:321
  11.7 8.1 %collective-permute-start.4 = (f32[230,128]{1,0:T(8,128)S(1)}, f32[230,128]{1,0:T(8,128)S(1)}, u32[]{:S(2)}, u32[]{:S(2)}) collective-permute-start(f32[230,128]{1,0:T(8,128)S(1)} %get-tuple-element.15), channel_id=1, source_target_pairs={{8,0},{16,8},{24,16},{0,24},{9,1},{17,9},{25,17},{1,25},{10,2},{18... | collective-permute-start | bytes 353288 | tf_op jit(solution)/shard_map/ppermute | solution.py:321
  13.3 7.1 %collective-permute-start.3 = (f32[120,128]{1,0:T(8,128)S(1)}, f32[120,128]{1,0:T(8,128)S(1)}, u32[]{:S(2)}, u32[]{:S(2)}) collective-permute-start(f32[120,128]{1,0:T(8,128)S(1)} %get-tuple-element.19), channel_id=1, source_target_pairs={{16,0},{24,8},{0,16},{8,24},{17,1},{25,9},{1,17},{9,25},{18,2},{26... | collective-permute-start | bytes 184328 | tf_op jit(solution)/shard_map/ppermute | solution.py:321
  13.9 6.0 %collective-permute-start.5 = (f32[70,128]{1,0:T(8,128)S(1)}, f32[70,128]{1,0:T(8,128)S(1)}, u32[]{:S(2)}, u32[]{:S(2)}) collective-permute-start(f32[70,128]{1,0:T(8,128)S(1)} %get-tuple-element.20), channel_id=1, source_target_pairs={{16,0},{24,8},{0,16},{8,24},{17,1},{25,9},{1,17},{9,25},{18,2},{26... | collective-permute-start | bytes 107528 | tf_op jit(solution)/shard_map/ppermute | solution.py:321
  21.7 3.7 %collective-permute-start.6 = (f32[16,128]{1,0:T(8,128)S(1)}, f32[16,128]{1,0:T(8,128)S(1)}, u32[]{:S(2)}, u32[]{:S(2)}) collective-permute-start(f32[16,128]{1,0:T(8,128)S(1)} %shard_map.31.refs_0_), channel_id=1, source_target_pairs={{4,0},{0,4},{5,1},{1,5},{6,2},{2,6},{7,3},{3,7},{12,8},{8,12},{13,... | collective-permute-start | bytes 24584 | tf_op jit(solution)/shard_map/ppermute | solution.py:321

commit v2 on v1

--- a/solution.py
+++ b/solution.py
@@ -68,32 +68,60 @@
     return [[(one if i == j else zero, zero) for j in range(3)] for i in range(rows)]
 
 
-def pivots(a):
-    size = [v[0] * v[0] + v[1] * v[1] for v in a]
-    first = jnp.logical_and(size[0] >= size[1], size[0] >= size[2])
-    last = jnp.logical_and(jnp.logical_not(first), size[2] > size[1])
-    return size, first, last
+def pivots(y):
+    sizes = [jnp.abs(v) for v in y]
+    middle, end = jnp.maximum(sizes[1], sizes[2]), jnp.maximum(sizes[3], sizes[4])
+    top = jnp.maximum(middle, end)
+    other = jnp.logical_and(jnp.logical_and(top >= 0.35, top <= 1.5), sizes[0] <= 0.4)
+    return jnp.logical_not(other), jnp.logical_and(other, end > middle)
 
 
 def pick(mask, p, q):
     return tuple(jnp.where(mask, u, v) for u, v in zip(p, q))
 
 
+VALUES = 8
+TINY, FAR = 1e-30, 1e15
+
+
+def projected(point):
+    c, rest = point[0], point[1:]
+    square = sum(v * v for v in rest)
+    below = c < 0.0
+    scale = jnp.where(below, 1.0 - c, 1.0) / jnp.where(below, jnp.maximum(square, TINY), 1.0 + c)
+    y = [v * scale for v in rest]
+    y[0] = jnp.where(jnp.logical_and(below, square < TINY), FAR, y[0])
+    return y
+
+
+def point_at(y):
+    square = sum(v * v for v in y)
+    inverse = 1.0 / (1.0 + square)
+    v = [(1.0 - square) * inverse, *(v * (2.0 * inverse) for v in y)]
+    return list(zip(v[0::2], v[1::2]))
+
+
 def sent(m):
-    a, b = m[0], m[1]
-    _, first, last = pivots(a)
-    return [e for v in (*a, pick(first, b[1], b[0]), pick(last, b[1], b[2])) for e in v]
+    y = projected([e for v in m[0] for e in v])
+    b = m[1]
+    first, last = pivots(y)
+    w = [*pick(first, b[1], b[0]), *pick(last, b[1], b[2])]
+    scale = lax.rsqrt(sum(v * v for v in w))
+    return y + projected([v * scale for v in w])
 
 
 def received(load):
-    v = [(load(2 * k), load(2 * k + 1)) for k in range(5)]
-    a, e, f = v[:3], v[3], v[4]
-    size, first, last = pivots(a)
+    v = [load(k) for k in range(VALUES)]
+    a = point_at(v[:5])
+    e, f = point_at(v[5:])
+    first, last = pivots(v[:5])
     p, q = pick(first, a[1], a[0]), pick(last, a[1], a[2])
     top = pick(first, a[0], pick(last, a[2], a[1]))
-    scale = -1.0 / jnp.maximum(jnp.maximum(size[0], size[1]), size[2])
+    scale = -1.0 / (top[0] * top[0] + top[1] * top[1])
     g = mul(add(mul_conj(e, p), mul_conj(f, q)), top)
     g = (g[0] * scale, g[1] * scale)
+    norm = lax.rsqrt(1.0 + g[0] * g[0] + g[1] * g[1])
+    e, f, g = [(u[0] * norm, u[1] * norm) for u in (e, f, g)]
     return [a, [pick(first, g, e), pick(first, e, pick(last, f, g)), pick(last, g, f)]]
 
 
@@ -147,7 +175,7 @@
         w = product_dagger(get(rows_of(u_ref, i, 8)[0]), after)
         put(rows_of(own_ref, i, 8)[1], w)
         send(flat_rows(near_ref, near, i, 8)[1], w)
-    for k in range(10):
+    for k in range(VALUES):
         far_ref[pl.ds(k * far, 2 * n), :] = near_ref[pl.ds(k * near, 2 * n), :]
         far_ref[pl.ds(k * far + 2 * n, 1), :] = near_ref[pl.ds(k * near + block + n, 1), :]
         edge_ref[pl.ds(k * edge, n), :] = near_ref[pl.ds(k * near, n, stride=n), :]
@@ -191,7 +219,7 @@
     keep(late * n + n, 1, first_of(pp, 1))
     g = received(flat_rows(far_ref, far, two, 1)[0])
     keep(late * n + n + 1, 1, product(first_of(pp, 1), completed(g)))
-    for k in range(10):
+    for k in range(VALUES):
         edge_ref[pl.ds(k * 2 * late, late), :] = late_ref[pl.ds(k * size, late, stride=n), :]
         edge_ref[pl.ds(k * 2 * late + late, late), :] = late_ref[pl.ds(k * size + late * n, late), :]
 
@@ -330,7 +358,7 @@
     flat = (18, block, lanes)
     own, near, far, edge = call(
         lambda *refs: gauge_kernel(n, *refs),
-        [(12, block + two, lanes)] + [(10 * rows, lanes) for rows in (block + two - 1, two + 1, two - 1)],
+        [(12, block + two, lanes)] + [(VALUES * rows, lanes) for rows in (block + two - 1, two + 1, two - 1)],
         [(18, block + 8, lanes), (12, block, lanes)],
         jnp.stack([link_x.reshape(flat), link_t.reshape(flat)]),
     )
@@ -338,7 +366,7 @@
     near_x, edge_x = ahead(near, "gx", 1), ahead(edge, "gx", 2)
     own2, near2, edge2 = call(
         lambda *refs: chain_kernel(n, *refs),
-        [(12 * size, lanes), (10 * size, lanes), (10 * 2 * late, lanes)],
+        [(12 * size, lanes), (VALUES * size, lanes), (VALUES * 2 * late, lanes)],
         [(18, 3 * n, lanes)],
         own,
         near_t,

time: 26.2 us -> 25.2 us (0.962)
  waiting for transfers between devices: 11.6 us -> 10.4 us
    ppermute x7, waiting for transfers between devices: 11.6 us -> 10.4 us  [ahead(): lax.ppermute(block, axis, [((i + distance) % count, i) for i in range(cou...]
  transfers between devices with their start and end apart: 7 -> 7, of which waited for: 3 -> 3; matrix products, arithmetic and copies ran while one was open for 0% -> 0% of each run, Pallas kernels for 2% -> 3%
where the time goes in v2:
time: 25.2 us; the launch traced here: 25.1 us
  starting transfers between devices  10.4 us (41%)
  waiting for transfers between devices  10.4 us (41%)
  Pallas kernels  3.27 us (13%)
  other arithmetic  1 us (4%)
    ppermute x7, waiting for transfers between devices, ahead(): lax.ppermute(block, axis, [((i + distance) % count, i) for i in range(cou...  10.4 us
    ppermute x7, starting transfers between devices, ahead(): lax.ppermute(block, axis, [((i + distance) % count, i) for i in range(cou...  10.4 us
    pallas_call x5, Pallas kernels, call(): pl.pallas_call(kernel, out_shape=[jax.ShapeDtypeStruct(s, jnp.float32) fo...  3.27 us
    another operation x1, other arithmetic, local(): jnp.stack([link_x.reshape(flat), link_t.reshape(flat)])  1 us
  transfers between devices with their start and end apart: 7, of which 3 were waited for; matrix products, arithmetic and copies ran while one was open for 0% of the time, Pallas kernels for 3%

profile of v2, /device:TPU:0, one launch (start us, length us, event | category | flops | bytes accessed | tf_op | source)
XLA Modules:
  0.0 25.1 jit_solution(1379757544695825771)
XLA Ops:
  0.0 1.0 %pad_maximum_fusion.refs_0_ = f32[2,18,16,128]{3,2,1,0:T(8,128)S(1)} fusion(f32[1,18,16,128]{3,2,1,0:T(8,128)} %bitcast.3, f32[1,18,16,128]{3,2,1,0:T(8,128)} %bitcast.4), kind=kLoop, calls=%fused_computation | loop fusion | flops 73728 | bytes 589824 | tf_op jit(solution)/shard_map/stack | solution.py:363
  1.0 0.3 shard_map.28
  1.3 5.1 %collective-permute-start = (f32[184,128]{1,0:T(8,128)S(1)}, f32[184,128]{1,0:T(8,128)S(1)}, u32[]{:S(2)}, u32[]{:S(2)}) collective-permute-start(f32[184,128]{1,0:T(8,128)S(1)} %get-tuple-element.15), channel_id=1, source_target_pairs={{1,0},{2,1},{3,2},{0,3},{5,4},{6,5},{7,6},{4,7},{9,8},{10,9},{11,1... | collective-permute-start | bytes 282632 | tf_op jit(solution)/shard_map/ppermute | solution.py:349
  6.4 0.0 collective-permute-start.1
  6.4 4.9 %collective-permute-done.1.refs_2_ = f32[72,128]{1,0:T(8,128)S(1)} collective-permute-done((f32[72,128]{1,0:T(8,128)S(1)}, f32[72,128]{1,0:T(8,128)S(1)}, u32[]{:S(2)}, u32[]{:S(2)}) %collective-permute-start.1) | collective-permute-done | bytes 36896 | tf_op jit(solution)/shard_map/ppermute | solution.py:349
  11.2 0.0 collective-permute-done.refs_1_
  11.2 0.4 %shard_map.29 = (f32[360,128]{1,0:T(8,128)S(1)}, f32[240,128]{1,0:T(8,128)S(1)}, f32[96,128]{1,0:T(8,128)S(1)}) custom-call(f32[12,24,128]{2,1,0:T(8,128)S(1)} %get-tuple-element.14.refs_0_, f32[184,128]{1,0:T(8,128)S(1)} %collective-permute-done.refs_1_, f32[72,128]{1,0:T(8,128)S(1)} %collective-permute-done.1.refs_2_), custom_call_target="tpu_custom_call" | custom-call | tf_op jit(solution)/shard_map/pallas_call | solution.py:337
  11.7 0.1 collective-permute-start.2
  11.7 1.6 %collective-permute-start.4 = (f32[184,128]{1,0:T(8,128)S(1)}, f32[184,128]{1,0:T(8,128)S(1)}, u32[]{:S(2)}, u32[]{:S(2)}) collective-permute-start(f32[184,128]{1,0:T(8,128)S(1)} %get-tuple-element.15), channel_id=1, source_target_pairs={{8,0},{16,8},{24,16},{0,24},{9,1},{17,9},{25,17},{1,25},{10,2},{18... | collective-permute-start | bytes 282632 | tf_op jit(solution)/shard_map/ppermute | solution.py:349
  13.4 0.5 %collective-permute-start.3 = (f32[96,128]{1,0:T(8,128)S(1)}, f32[96,128]{1,0:T(8,128)S(1)}, u32[]{:S(2)}, u32[]{:S(2)}) collective-permute-start(f32[96,128]{1,0:T(8,128)S(1)} %get-tuple-element.19), channel_id=1, source_target_pairs={{16,0},{24,8},{0,16},{8,24},{17,1},{25,9},{1,17},{9,25},{18,2},{26... | collective-permute-start | bytes 147464 | tf_op jit(solution)/shard_map/ppermute | solution.py:349
  13.9 1.5 %collective-permute-start.5 = (f32[56,128]{1,0:T(8,128)S(1)}, f32[56,128]{1,0:T(8,128)S(1)}, u32[]{:S(2)}, u32[]{:S(2)}) collective-permute-start(f32[56,128]{1,0:T(8,128)S(1)} %get-tuple-element.20), channel_id=1, source_target_pairs={{16,0},{24,8},{0,16},{8,24},{17,1},{25,9},{1,17},{9,25},{18,2},{26... | collective-permute-start | bytes 86024 | tf_op jit(solution)/shard_map/ppermute | solution.py:349
  15.4 3.4 %collective-permute-done.5.refs_2_ = f32[56,128]{1,0:T(8,128)S(1)} collective-permute-done((f32[56,128]{1,0:T(8,128)S(1)}, f32[56,128]{1,0:T(8,128)S(1)}, u32[]{:S(2)}, u32[]{:S(2)}) %collective-permute-start.5) | collective-permute-done | bytes 28704 | tf_op jit(solution)/shard_map/ppermute | solution.py:349
  18.8 0.0 collective-permute-done.4.refs_1_
  18.8 0.7 %shard_map.30 = (f32[108,16,128]{2,1,0:T(8,128)S(1)}, f32[8,128]{1,0:T(8,128)S(1)}) custom-call(f32[12,24,128]{2,1,0:T(8,128)S(1)} %get-tuple-element.14.refs_0_, f32[184,128]{1,0:T(8,128)S(1)} %collective-permute-done.4.refs_1_, f32[56,128]{1,0:T(8,128)S(1)} %collective-permute-done.5.refs_2_), custom_call_target="tpu_custom_call" | custom-call | tf_op jit(solution)/shard_map/pallas_call | solution.py:337
  19.4 0.0 collective-permute-done.3.refs_2_
  19.4 0.0 collective-permute-done.2.refs_1_
  19.4 1.2 %shard_map.31.refs_0_ = f32[16,128]{1,0:T(8,128)S(1)} custom-call(f32[360,128]{1,0:T(8,128)S(1)} %get-tuple-element.17.refs_0_, f32[240,128]{1,0:T(8,128)S(1)} %collective-permute-done.2.refs_1_, f32[96,128]{1,0:T(8,128)S(1)} %collective-permute-done.3.refs_2_, f32[108,16,128]{2,1,0:T(8,128)S(1)} %get-tuple-element.21.refs_3_, ...), custom_call_target="tpu_custom_call" | custom-call | tf_op jit(solution)/shard_map/pallas_call | solution.py:337
  20.7 1.5 %collective-permute-start.6 = (f32[16,128]{1,0:T(8,128)S(1)}, f32[16,128]{1,0:T(8,128)S(1)}, u32[]{:S(2)}, u32[]{:S(2)}) collective-permute-start(f32[16,128]{1,0:T(8,128)S(1)} %shard_map.31.refs_0_), channel_id=1, source_target_pairs={{4,0},{0,4},{5,1},{1,5},{6,2},{2,6},{7,3},{3,7},{12,8},{8,12},{13,... | collective-permute-start | bytes 24584 | tf_op jit(solution)/shard_map/ppermute | solution.py:349
  22.2 2.2 %collective-permute-done.6.refs_1_ = f32[16,128]{1,0:T(8,128)S(1)} collective-permute-done((f32[16,128]{1,0:T(8,128)S(1)}, f32[16,128]{1,0:T(8,128)S(1)}, u32[]{:S(2)}, u32[]{:S(2)}) %collective-permute-start.6) | collective-permute-done | bytes 8224 | tf_op jit(solution)/shard_map/ppermute | solution.py:349
  24.4 0.7 %shard_map.32 = f32[6,4,4,6]{3,2,1,0:T(4,128)} custom-call(f32[16,128]{1,0:T(8,128)S(1)} %shard_map.31.refs_0_, f32[16,128]{1,0:T(8,128)S(1)} %collective-permute-done.6.refs_1_), custom_call_target="tpu_custom_call" | custom-call | tf_op jit(solution)/shard_map/pallas_call | solution.py:337
Async XLA Ops:
  1.3 10.0 %collective-permute-start = (f32[184,128]{1,0:T(8,128)S(1)}, f32[184,128]{1,0:T(8,128)S(1)}, u32[]{:S(2)}, u32[]{:S(2)}) collective-permute-start(f32[184,128]{1,0:T(8,128)S(1)} %get-tuple-element.15), channel_id=1, source_target_pairs={{1,0},{2,1},{3,2},{0,3},{5,4},{6,5},{7,6},{4,7},{9,8},{10,9},{11,1... | collective-permute-start | bytes 282632 | tf_op jit(solution)/shard_map/ppermute | solution.py:349
  6.4 4.9 %collective-permute-start.1 = (f32[72,128]{1,0:T(8,128)S(1)}, f32[72,128]{1,0:T(8,128)S(1)}, u32[]{:S(2)}, u32[]{:S(2)}) collective-permute-start(f32[72,128]{1,0:T(8,128)S(1)} %get-tuple-element.16), channel_id=1, source_target_pairs={{2,0},{3,1},{0,2},{1,3},{6,4},{7,5},{4,6},{5,7},{10,8},{11,9},{8,1... | collective-permute-start | bytes 110600 | tf_op jit(solution)/shard_map/ppermute | solution.py:349
  11.7 7.8 %collective-permute-start.2 = (f32[240,128]{1,0:T(8,128)S(1)}, f32[240,128]{1,0:T(8,128)S(1)}, u32[]{:S(2)}, u32[]{:S(2)}) collective-permute-start(f32[240,128]{1,0:T(8,128)S(1)} %get-tuple-element.18), channel_id=1, source_target_pairs={{8,0},{16,8},{24,16},{0,24},{9,1},{17,9},{25,17},{1,25},{10,2},{18... | collective-permute-start | bytes 368648 | tf_op jit(solution)/shard_map/ppermute | solution.py:349
  11.7 7.0 %collective-permute-start.4 = (f32[184,128]{1,0:T(8,128)S(1)}, f32[184,128]{1,0:T(8,128)S(1)}, u32[]{:S(2)}, u32[]{:S(2)}) collective-permute-start(f32[184,128]{1,0:T(8,128)S(1)} %get-tuple-element.15), channel_id=1, source_target_pairs={{8,0},{16,8},{24,16},{0,24},{9,1},{17,9},{25,17},{1,25},{10,2},{18... | collective-permute-start | bytes 282632 | tf_op jit(solution)/shard_map/ppermute | solution.py:349
  13.4 6.1 %collective-permute-start.3 = (f32[96,128]{1,0:T(8,128)S(1)}, f32[96,128]{1,0:T(8,128)S(1)}, u32[]{:S(2)}, u32[]{:S(2)}) collective-permute-start(f32[96,128]{1,0:T(8,128)S(1)} %get-tuple-element.19), channel_id=1, source_target_pairs={{16,0},{24,8},{0,16},{8,24},{17,1},{25,9},{1,17},{9,25},{18,2},{26... | collective-permute-start | bytes 147464 | tf_op jit(solution)/shard_map/ppermute | solution.py:349
  13.9 4.9 %collective-permute-start.5 = (f32[56,128]{1,0:T(8,128)S(1)}, f32[56,128]{1,0:T(8,128)S(1)}, u32[]{:S(2)}, u32[]{:S(2)}) collective-permute-start(f32[56,128]{1,0:T(8,128)S(1)} %get-tuple-element.20), channel_id=1, source_target_pairs={{16,0},{24,8},{0,16},{8,24},{17,1},{25,9},{1,17},{9,25},{18,2},{26... | collective-permute-start | bytes 86024 | tf_op jit(solution)/shard_map/ppermute | solution.py:349
  20.7 3.7 %collective-permute-start.6 = (f32[16,128]{1,0:T(8,128)S(1)}, f32[16,128]{1,0:T(8,128)S(1)}, u32[]{:S(2)}, u32[]{:S(2)}) collective-permute-start(f32[16,128]{1,0:T(8,128)S(1)} %shard_map.31.refs_0_), channel_id=1, source_target_pairs={{4,0},{0,4},{5,1},{1,5},{6,2},{2,6},{7,3},{3,7},{12,8},{8,12},{13,... | collective-permute-start | bytes 24584 | tf_op jit(solution)/shard_map/ppermute | solution.py:349

commit v3 on v2

--- a/solution.py
+++ b/solution.py
@@ -163,12 +163,9 @@
         put(rows_of(u_ref, t * n, n)[1], product(g, full) if t else full[:2])
         step = raw(1, t, 3)
         g = product(g, step) if t else step[:2]
-    put(rows_of(own_ref, block + n, n)[1], g)
-    send(flat_rows(near_ref, near, block, n)[1], g)
-    g = get(rows_of(g_ref, 0, n, n)[0])
     put(rows_of(own_ref, block, n)[1], g)
-    g = [[tuple(e[1:] for e in v) for v in row] for row in g]
-    send(flat_rows(near_ref, near, block + n, n - 1)[1], g)
+    put(rows_of(own_ref, block + n, n - 1)[1], get(rows_of(g_ref, n, n - 1, n)[0]))
+    send(flat_rows(near_ref, near, block, 2 * n - 1)[1], get(rows_of(own_ref, block, 2 * n - 1)[0]))
     last = lax.broadcasted_iota(jnp.int32, (8, lanes), 0) % n == n - 1
     for i in range(0, block, 8):
         after = where(last, unit((8, lanes), 3), get(rows_of(g_ref, i + 1, 8)[0], 3))
@@ -203,22 +200,24 @@
     def first_of(p, count):
         return [[tuple(jnp.broadcast_to(e[0:1], (count, lanes)) for e in q) for q in row] for row in p]
 
-    p = get(rows_of(own_ref, block + n, n)[0])
+    p = get(rows_of(own_ref, block, n)[0])
     p_next = received(flat_rows(near_ref, near, block, n)[0])
     pp = product(p, completed(p_next))
+    hold = lambda first, count, m: put(flat_rows(out_ref, size, first, count)[1], m)
+    hold(late * n, 1, first_of(p, 1))
+    g = received(flat_rows(near_ref, near, block + n, n - 1)[0])
+    hold(late * n + 1, n - 1, product(first_of(p, n - 1), completed(g)))
+    hold(late * n + n, 1, first_of(pp, 1))
+    g = received(flat_rows(far_ref, far, two, 1)[0])
+    hold(late * n + n + 1, 1, product(first_of(pp, 1), completed(g)))
     left, right = spread(p)
     for i in range(0, block, 8):
         w = received(flat_rows(near_ref, near, i, 8)[0])
         keep(i, 8, product_dagger(product(left, completed(w)), right))
-    keep(late * n, 1, first_of(p, 1))
-    g = received(flat_rows(near_ref, near, block + n, n - 1)[0])
-    keep(late * n + 1, n - 1, product(first_of(p, n - 1), completed(g)))
     left, right = spread(pp)
     w = received(flat_rows(far_ref, far, 0, two)[0])
     keep(block, two, product_dagger(product(left, completed(w)), right))
-    keep(late * n + n, 1, first_of(pp, 1))
-    g = received(flat_rows(far_ref, far, two, 1)[0])
-    keep(late * n + n + 1, 1, product(first_of(pp, 1), completed(g)))
+    send(flat_rows(late_ref, size, late * n, late)[1], get(flat_rows(out_ref, size, late * n, late)[0]))
     for k in range(VALUES):
         edge_ref[pl.ds(k * 2 * late, late), :] = late_ref[pl.ds(k * size, late, stride=n), :]
         edge_ref[pl.ds(k * 2 * late + late, late), :] = late_ref[pl.ds(k * size + late * n, late), :]
@@ -231,25 +230,25 @@
     lanes = a_ref.shape[-1]
     for ref, g in zip((a_ref, b_ref), closing):
         load, keep = rows_of(ref, PAD + n - 1, times, n)
-        put(keep, product_dagger(get(load), completed(g)))
+        put(keep, completed(product_dagger(get(load), completed(g))))
     x_of = lax.broadcasted_iota(jnp.int32, (8, lanes), 0) % n
 
     def window(k, i):
-        own = lambda shift: get(rows_of(a_ref, PAD + i + shift, 8)[0])
-        after = lambda shift: get(rows_of(b_ref, PAD + i + shift, 8)[0])
+        own = lambda shift: get(rows_of(a_ref, PAD + i + shift, 8)[0], 3)
+        after = lambda shift: get(rows_of(b_ref, PAD + i + shift, 8)[0], 3)
         if k == 0:
             return own(0)
         if k < n:
             return where(x_of < n - k, own(k), after(k - n))
         if k == n:
             return after(0)
-        return where(x_of < n - 1, after(1), get(rows_of(c_ref, i, 8)[0]))
+        return where(x_of < n - 1, after(1), get(rows_of(c_ref, i, 8)[0], 3))
 
     for i in range(0, times * n, 8):
-        s = window(0, i)
+        s = window(0, i)[:2]
         for r in range(RMAX):
             if r:
-                s = product(s, completed(window(r, i)))
+                s = product(s, window(r, i))
             put(lambda c, v: store(r * 18 + c, i, v), completed(s))
 
 
@@ -267,9 +266,9 @@
     block = n * n
     near, edge = block + 2 * n - 1, 2 * n - 1
     for i in range(0, block, 8):
-        put(rows_of(a_ref, PAD + i, 8)[1], get(rows_of(own_ref, i, 8)[0]))
-        put(rows_of(b_ref, PAD + i, 8)[1], received(flat_rows(near_ref, near, i, 8)[0]))
-    put(rows_of(c_ref, n - 1, n, n)[1], received(flat_rows(far_ref, edge, 0, n)[0]))
+        put(rows_of(a_ref, PAD + i, 8)[1], completed(get(rows_of(own_ref, i, 8)[0])))
+        put(rows_of(b_ref, PAD + i, 8)[1], completed(received(flat_rows(near_ref, near, i, 8)[0])))
+    put(rows_of(c_ref, n - 1, n, n)[1], completed(received(flat_rows(far_ref, edge, 0, n)[0])))
     closing = []
     for k, load in enumerate((flat_rows(near_ref, near, block + n, n - 1), flat_rows(far_ref, edge, n, n - 1))):
         put(rows_of(g_ref, 0, 1, offset=12 * k)[1], unit((1, lanes)))
@@ -294,9 +293,9 @@
     late = n + 2
     size = late * (n + 1)
     for i in range(0, late * n, 8):
-        put(rows_of(a_ref, PAD + i, 8)[1], get(flat_rows(own_ref, size, i, 8)[0]))
-        put(rows_of(b_ref, PAD + i, 8)[1], received(flat_rows(near_ref, size, i, 8)[0]))
-    put(rows_of(c_ref, n - 1, late, n)[1], received(flat_rows(far_ref, 2 * late, 0, late)[0]))
+        put(rows_of(a_ref, PAD + i, 8)[1], completed(get(flat_rows(own_ref, size, i, 8)[0])))
+        put(rows_of(b_ref, PAD + i, 8)[1], completed(received(flat_rows(near_ref, size, i, 8)[0])))
+    put(rows_of(c_ref, n - 1, late, n)[1], completed(received(flat_rows(far_ref, 2 * late, 0, late)[0])))
     closing = [
         received(flat_rows(near_ref, size, late * n, late)[0]),
         received(flat_rows(far_ref, 2 * late, late, late)[0]),
@@ -374,7 +373,7 @@
     )
     near2_x, edge2_x = ahead(near2, "gx", 1), ahead(edge2, "gx", 2)
     transport = (RMAX * 18, block, lanes)
-    spaces = lambda rows: [(12, rows + 2 * PAD, lanes), (12, rows + 2 * PAD, lanes), (12, rows, lanes)]
+    spaces = lambda rows: [(18, rows + 2 * PAD, lanes), (18, rows + 2 * PAD, lanes), (18, rows, lanes)]
     early, packed = call(
         lambda *refs: early_kernel(n, *refs),
         [transport, (8, lanes)],

time: 25.2 us -> 25.2 us (level)
  no operation moved by 1% of the time
where the time goes in v3:
time: 25.2 us; the launch traced here: 25 us
  starting transfers between devices  10.4 us (41%)
  waiting for transfers between devices  10.4 us (41%)
  Pallas kernels  3.24 us (13%)
  other arithmetic  1 us (4%)
    ppermute x7, waiting for transfers between devices, ahead(): lax.ppermute(block, axis, [((i + distance) % count, i) for i in range(cou...  10.4 us
    ppermute x7, starting transfers between devices, ahead(): lax.ppermute(block, axis, [((i + distance) % count, i) for i in range(cou...  10.4 us
    pallas_call x5, Pallas kernels, call(): pl.pallas_call(kernel, out_shape=[jax.ShapeDtypeStruct(s, jnp.float32) fo...  3.24 us
    another operation x1, other arithmetic, local(): jnp.stack([link_x.reshape(flat), link_t.reshape(flat)])  1 us
  transfers between devices with their start and end apart: 7, of which 3 were waited for; matrix products, arithmetic and copies ran while one was open for 0% of the time, Pallas kernels for 3%

profile of v3, /device:TPU:0, one launch (start us, length us, event | category | flops | bytes accessed | tf_op | source)
XLA Modules:
  0.0 25.0 jit_solution(18137775782272240108)
XLA Ops:
  0.0 1.0 %pad_maximum_fusion.refs_0_ = f32[2,18,16,128]{3,2,1,0:T(8,128)S(1)} fusion(f32[1,18,16,128]{3,2,1,0:T(8,128)} %bitcast.3, f32[1,18,16,128]{3,2,1,0:T(8,128)} %bitcast.4), kind=kLoop, calls=%fused_computation | loop fusion | flops 73728 | bytes 589824 | tf_op jit(solution)/shard_map/stack | solution.py:362
  1.0 0.2 shard_map.28
  1.3 5.1 %collective-permute-start = (f32[184,128]{1,0:T(8,128)S(1)}, f32[184,128]{1,0:T(8,128)S(1)}, u32[]{:S(2)}, u32[]{:S(2)}) collective-permute-start(f32[184,128]{1,0:T(8,128)S(1)} %get-tuple-element.15), channel_id=1, source_target_pairs={{1,0},{2,1},{3,2},{0,3},{5,4},{6,5},{7,6},{4,7},{9,8},{10,9},{11,1... | collective-permute-start | bytes 282632 | tf_op jit(solution)/shard_map/ppermute | solution.py:348
  6.4 0.0 collective-permute-start.1
  6.4 4.9 %collective-permute-done.1.refs_2_ = f32[72,128]{1,0:T(8,128)S(1)} collective-permute-done((f32[72,128]{1,0:T(8,128)S(1)}, f32[72,128]{1,0:T(8,128)S(1)}, u32[]{:S(2)}, u32[]{:S(2)}) %collective-permute-start.1) | collective-permute-done | bytes 36896 | tf_op jit(solution)/shard_map/ppermute | solution.py:348
  11.2 0.0 collective-permute-done.refs_1_
  11.2 0.4 %shard_map.29 = (f32[360,128]{1,0:T(8,128)S(1)}, f32[240,128]{1,0:T(8,128)S(1)}, f32[96,128]{1,0:T(8,128)S(1)}) custom-call(f32[12,24,128]{2,1,0:T(8,128)S(1)} %get-tuple-element.14.refs_0_, f32[184,128]{1,0:T(8,128)S(1)} %collective-permute-done.refs_1_, f32[72,128]{1,0:T(8,128)S(1)} %collective-permute-done.1.refs_2_), custom_call_target="tpu_custom_call" | custom-call | tf_op jit(solution)/shard_map/pallas_call | solution.py:336
  11.6 0.1 collective-permute-start.2
  11.7 1.6 %collective-permute-start.4 = (f32[184,128]{1,0:T(8,128)S(1)}, f32[184,128]{1,0:T(8,128)S(1)}, u32[]{:S(2)}, u32[]{:S(2)}) collective-permute-start(f32[184,128]{1,0:T(8,128)S(1)} %get-tuple-element.15), channel_id=1, source_target_pairs={{8,0},{16,8},{24,16},{0,24},{9,1},{17,9},{25,17},{1,25},{10,2},{18... | collective-permute-start | bytes 282632 | tf_op jit(solution)/shard_map/ppermute | solution.py:348
  13.3 0.5 %collective-permute-start.3 = (f32[96,128]{1,0:T(8,128)S(1)}, f32[96,128]{1,0:T(8,128)S(1)}, u32[]{:S(2)}, u32[]{:S(2)}) collective-permute-start(f32[96,128]{1,0:T(8,128)S(1)} %get-tuple-element.19), channel_id=1, source_target_pairs={{16,0},{24,8},{0,16},{8,24},{17,1},{25,9},{1,17},{9,25},{18,2},{26... | collective-permute-start | bytes 147464 | tf_op jit(solution)/shard_map/ppermute | solution.py:348
  13.8 1.5 %collective-permute-start.5 = (f32[56,128]{1,0:T(8,128)S(1)}, f32[56,128]{1,0:T(8,128)S(1)}, u32[]{:S(2)}, u32[]{:S(2)}) collective-permute-start(f32[56,128]{1,0:T(8,128)S(1)} %get-tuple-element.20), channel_id=1, source_target_pairs={{16,0},{24,8},{0,16},{8,24},{17,1},{25,9},{1,17},{9,25},{18,2},{26... | collective-permute-start | bytes 86024 | tf_op jit(solution)/shard_map/ppermute | solution.py:348
  15.3 3.4 %collective-permute-done.5.refs_2_ = f32[56,128]{1,0:T(8,128)S(1)} collective-permute-done((f32[56,128]{1,0:T(8,128)S(1)}, f32[56,128]{1,0:T(8,128)S(1)}, u32[]{:S(2)}, u32[]{:S(2)}) %collective-permute-start.5) | collective-permute-done | bytes 28704 | tf_op jit(solution)/shard_map/ppermute | solution.py:348
  18.7 0.0 collective-permute-done.4.refs_1_
  18.7 0.7 %shard_map.30 = (f32[108,16,128]{2,1,0:T(8,128)S(1)}, f32[8,128]{1,0:T(8,128)S(1)}) custom-call(f32[12,24,128]{2,1,0:T(8,128)S(1)} %get-tuple-element.14.refs_0_, f32[184,128]{1,0:T(8,128)S(1)} %collective-permute-done.4.refs_1_, f32[56,128]{1,0:T(8,128)S(1)} %collective-permute-done.5.refs_2_), custom_call_target="tpu_custom_call" | custom-call | tf_op jit(solution)/shard_map/pallas_call | solution.py:336
  19.4 0.0 collective-permute-done.3.refs_2_
  19.4 0.0 collective-permute-done.2.refs_1_
  19.4 1.2 %shard_map.31.refs_0_ = f32[16,128]{1,0:T(8,128)S(1)} custom-call(f32[360,128]{1,0:T(8,128)S(1)} %get-tuple-element.17.refs_0_, f32[240,128]{1,0:T(8,128)S(1)} %collective-permute-done.2.refs_1_, f32[96,128]{1,0:T(8,128)S(1)} %collective-permute-done.3.refs_2_, f32[108,16,128]{2,1,0:T(8,128)S(1)} %get-tuple-element.21.refs_3_, ...), custom_call_target="tpu_custom_call" | custom-call | tf_op jit(solution)/shard_map/pallas_call | solution.py:336
  20.6 1.5 %collective-permute-start.6 = (f32[16,128]{1,0:T(8,128)S(1)}, f32[16,128]{1,0:T(8,128)S(1)}, u32[]{:S(2)}, u32[]{:S(2)}) collective-permute-start(f32[16,128]{1,0:T(8,128)S(1)} %shard_map.31.refs_0_), channel_id=1, source_target_pairs={{4,0},{0,4},{5,1},{1,5},{6,2},{2,6},{7,3},{3,7},{12,8},{8,12},{13,... | collective-permute-start | bytes 24584 | tf_op jit(solution)/shard_map/ppermute | solution.py:348
  22.2 2.2 %collective-permute-done.6.refs_1_ = f32[16,128]{1,0:T(8,128)S(1)} collective-permute-done((f32[16,128]{1,0:T(8,128)S(1)}, f32[16,128]{1,0:T(8,128)S(1)}, u32[]{:S(2)}, u32[]{:S(2)}) %collective-permute-start.6) | collective-permute-done | bytes 8224 | tf_op jit(solution)/shard_map/ppermute | solution.py:348
  24.3 0.7 %shard_map.32 = f32[6,4,4,6]{3,2,1,0:T(4,128)} custom-call(f32[16,128]{1,0:T(8,128)S(1)} %shard_map.31.refs_0_, f32[16,128]{1,0:T(8,128)S(1)} %collective-permute-done.6.refs_1_), custom_call_target="tpu_custom_call" | custom-call | tf_op jit(solution)/shard_map/pallas_call | solution.py:336
Async XLA Ops:
  1.3 10.0 %collective-permute-start = (f32[184,128]{1,0:T(8,128)S(1)}, f32[184,128]{1,0:T(8,128)S(1)}, u32[]{:S(2)}, u32[]{:S(2)}) collective-permute-start(f32[184,128]{1,0:T(8,128)S(1)} %get-tuple-element.15), channel_id=1, source_target_pairs={{1,0},{2,1},{3,2},{0,3},{5,4},{6,5},{7,6},{4,7},{9,8},{10,9},{11,1... | collective-permute-start | bytes 282632 | tf_op jit(solution)/shard_map/ppermute | solution.py:348
  6.4 4.9 %collective-permute-start.1 = (f32[72,128]{1,0:T(8,128)S(1)}, f32[72,128]{1,0:T(8,128)S(1)}, u32[]{:S(2)}, u32[]{:S(2)}) collective-permute-start(f32[72,128]{1,0:T(8,128)S(1)} %get-tuple-element.16), channel_id=1, source_target_pairs={{2,0},{3,1},{0,2},{1,3},{6,4},{7,5},{4,6},{5,7},{10,8},{11,9},{8,1... | collective-permute-start | bytes 110600 | tf_op jit(solution)/shard_map/ppermute | solution.py:348
  11.6 7.8 %collective-permute-start.2 = (f32[240,128]{1,0:T(8,128)S(1)}, f32[240,128]{1,0:T(8,128)S(1)}, u32[]{:S(2)}, u32[]{:S(2)}) collective-permute-start(f32[240,128]{1,0:T(8,128)S(1)} %get-tuple-element.18), channel_id=1, source_target_pairs={{8,0},{16,8},{24,16},{0,24},{9,1},{17,9},{25,17},{1,25},{10,2},{18... | collective-permute-start | bytes 368648 | tf_op jit(solution)/shard_map/ppermute | solution.py:348
  11.7 7.0 %collective-permute-start.4 = (f32[184,128]{1,0:T(8,128)S(1)}, f32[184,128]{1,0:T(8,128)S(1)}, u32[]{:S(2)}, u32[]{:S(2)}) collective-permute-start(f32[184,128]{1,0:T(8,128)S(1)} %get-tuple-element.15), channel_id=1, source_target_pairs={{8,0},{16,8},{24,16},{0,24},{9,1},{17,9},{25,17},{1,25},{10,2},{18... | collective-permute-start | bytes 282632 | tf_op jit(solution)/shard_map/ppermute | solution.py:348
  13.3 6.1 %collective-permute-start.3 = (f32[96,128]{1,0:T(8,128)S(1)}, f32[96,128]{1,0:T(8,128)S(1)}, u32[]{:S(2)}, u32[]{:S(2)}) collective-permute-start(f32[96,128]{1,0:T(8,128)S(1)} %get-tuple-element.19), channel_id=1, source_target_pairs={{16,0},{24,8},{0,16},{8,24},{17,1},{25,9},{1,17},{9,25},{18,2},{26... | collective-permute-start | bytes 147464 | tf_op jit(solution)/shard_map/ppermute | solution.py:348
  13.8 4.9 %collective-permute-start.5 = (f32[56,128]{1,0:T(8,128)S(1)}, f32[56,128]{1,0:T(8,128)S(1)}, u32[]{:S(2)}, u32[]{:S(2)}) collective-permute-start(f32[56,128]{1,0:T(8,128)S(1)} %get-tuple-element.20), channel_id=1, source_target_pairs={{16,0},{24,8},{0,16},{8,24},{17,1},{25,9},{1,17},{9,25},{18,2},{26... | collective-permute-start | bytes 86024 | tf_op jit(solution)/shard_map/ppermute | solution.py:348
  20.6 3.7 %collective-permute-start.6 = (f32[16,128]{1,0:T(8,128)S(1)}, f32[16,128]{1,0:T(8,128)S(1)}, u32[]{:S(2)}, u32[]{:S(2)}) collective-permute-start(f32[16,128]{1,0:T(8,128)S(1)} %shard_map.31.refs_0_), channel_id=1, source_target_pairs={{4,0},{0,4},{5,1},{1,5},{6,2},{2,6},{7,3},{3,7},{12,8},{8,12},{13,... | collective-permute-start | bytes 24584 | tf_op jit(solution)/shard_map/ppermute | solution.py:348

commit v4 on v3

--- a/solution.py
+++ b/solution.py
@@ -230,7 +230,7 @@
     lanes = a_ref.shape[-1]
     for ref, g in zip((a_ref, b_ref), closing):
         load, keep = rows_of(ref, PAD + n - 1, times, n)
-        put(keep, completed(product_dagger(get(load), completed(g))))
+        put(keep, completed(product_dagger(get(load), g)))
     x_of = lax.broadcasted_iota(jnp.int32, (8, lanes), 0) % n
 
     def window(k, i):
@@ -273,7 +273,7 @@
     for k, load in enumerate((flat_rows(near_ref, near, block + n, n - 1), flat_rows(far_ref, edge, n, n - 1))):
         put(rows_of(g_ref, 0, 1, offset=12 * k)[1], unit((1, lanes)))
         put(rows_of(g_ref, 1, n - 1, offset=12 * k)[1], received(load[0]))
-        closing.append(get(rows_of(g_ref, 0, n, offset=12 * k)[0]))
+        closing.append(completed(get(rows_of(g_ref, 0, n, offset=12 * k)[0])))
 
     def store(c, i, v):
         s_ref[c, pl.ds(i, 8), :] = v
@@ -288,17 +288,22 @@
     out_ref[...] = packed
 
 
-def late_kernel(n, own_ref, near_ref, far_ref, early_ref, packed_ref, out_ref, a_ref, b_ref, c_ref, s_ref):
+def edge_kernel(n, far_ref, c_ref, g_ref):
+    late = n + 2
+    put(rows_of(c_ref, n - 1, late, n)[1], completed(received(flat_rows(far_ref, 2 * late, 0, late)[0])))
+    put(rows_of(g_ref, 0, late)[1], completed(received(flat_rows(far_ref, 2 * late, late, late)[0])))
+
+
+def late_kernel(n, own_ref, near_ref, c_ref, g_ref, early_ref, packed_ref, out_ref, a_ref, b_ref, s_ref):
     lanes = own_ref.shape[-1]
     late = n + 2
     size = late * (n + 1)
     for i in range(0, late * n, 8):
         put(rows_of(a_ref, PAD + i, 8)[1], completed(get(flat_rows(own_ref, size, i, 8)[0])))
         put(rows_of(b_ref, PAD + i, 8)[1], completed(received(flat_rows(near_ref, size, i, 8)[0])))
-    put(rows_of(c_ref, n - 1, late, n)[1], completed(received(flat_rows(far_ref, 2 * late, 0, late)[0])))
     closing = [
-        received(flat_rows(near_ref, size, late * n, late)[0]),
-        received(flat_rows(far_ref, 2 * late, late, late)[0]),
+        completed(received(flat_rows(near_ref, size, late * n, late)[0])),
+        get(rows_of(g_ref, 0, late)[0], 3),
     ]
 
     def store(c, i, v):
@@ -382,13 +387,17 @@
         near_x,
         edge_x,
     )
+    after, close = call(
+        lambda *refs: edge_kernel(n, *refs), [(18, late * n, lanes), (18, 8, lanes)], [], edge2_x
+    )
     (packed,) = call(
         lambda *refs: late_kernel(n, *refs),
         [(16, lanes)],
-        [*spaces(late * n), (RMAX * 18, (late + 1) * n, lanes)],
+        [*spaces(late * n)[:2], (RMAX * 18, (late + 1) * n, lanes)],
         own2,
         near2_x,
-        edge2_x,
+        after,
+        close,
         early,
         packed,
     )

time: 25.2 us -> 25.2 us (level)
    pallas_call x5 -> x6, Pallas kernels: 3.24 us -> 3.26 us  [call(): pl.pallas_call(kernel, out_shape=[jax.ShapeDtypeStruct(s, jnp.float32) fo...]
where the time goes in v4:
time: 25.2 us; the launch traced here: 25.1 us
  starting transfers between devices  10.4 us (41%)
  waiting for transfers between devices  10.4 us (41%)
  Pallas kernels  3.26 us (13%)
  other arithmetic  1 us (4%)
    ppermute x7, waiting for transfers between devices, ahead(): lax.ppermute(block, axis, [((i + distance) % count, i) for i in range(cou...  10.4 us
    ppermute x7, starting transfers between devices, ahead(): lax.ppermute(block, axis, [((i + distance) % count, i) for i in range(cou...  10.4 us
    pallas_call x6, Pallas kernels, call(): pl.pallas_call(kernel, out_shape=[jax.ShapeDtypeStruct(s, jnp.float32) fo...  3.26 us
    another operation x1, other arithmetic, local(): jnp.stack([link_x.reshape(flat), link_t.reshape(flat)])  1 us
  transfers between devices with their start and end apart: 7, of which 3 were waited for; matrix products, arithmetic and copies ran while one was open for 0% of the time, Pallas kernels for 3%

profile of v4, /device:TPU:0, one launch (start us, length us, event | category | flops | bytes accessed | tf_op | source)
XLA Modules:
  0.0 25.1 jit_solution(4030272121425822088)
XLA Ops:
  0.0 1.0 %pad_maximum_fusion.refs_0_ = f32[2,18,16,128]{3,2,1,0:T(8,128)S(1)} fusion(f32[1,18,16,128]{3,2,1,0:T(8,128)} %bitcast.3, f32[1,18,16,128]{3,2,1,0:T(8,128)} %bitcast.4), kind=kLoop, calls=%fused_computation | loop fusion | flops 73728 | bytes 589824 | tf_op jit(solution)/shard_map/stack | solution.py:367
  1.0 0.2 shard_map.28
  1.3 5.1 %collective-permute-start = (f32[184,128]{1,0:T(8,128)S(1)}, f32[184,128]{1,0:T(8,128)S(1)}, u32[]{:S(2)}, u32[]{:S(2)}) collective-permute-start(f32[184,128]{1,0:T(8,128)S(1)} %get-tuple-element.17), channel_id=1, source_target_pairs={{1,0},{2,1},{3,2},{0,3},{5,4},{6,5},{7,6},{4,7},{9,8},{10,9},{11,1... | collective-permute-start | bytes 282632 | tf_op jit(solution)/shard_map/ppermute | solution.py:353
  6.4 0.0 collective-permute-start.1
  6.4 4.9 %collective-permute-done.1.refs_2_ = f32[72,128]{1,0:T(8,128)S(1)} collective-permute-done((f32[72,128]{1,0:T(8,128)S(1)}, f32[72,128]{1,0:T(8,128)S(1)}, u32[]{:S(2)}, u32[]{:S(2)}) %collective-permute-start.1) | collective-permute-done | bytes 36896 | tf_op jit(solution)/shard_map/ppermute | solution.py:353
  11.2 0.0 collective-permute-done.refs_1_
  11.2 0.4 %shard_map.29 = (f32[360,128]{1,0:T(8,128)S(1)}, f32[240,128]{1,0:T(8,128)S(1)}, f32[96,128]{1,0:T(8,128)S(1)}) custom-call(f32[12,24,128]{2,1,0:T(8,128)S(1)} %get-tuple-element.16.refs_0_, f32[184,128]{1,0:T(8,128)S(1)} %collective-permute-done.refs_1_, f32[72,128]{1,0:T(8,128)S(1)} %collective-permute-done.1.refs_2_), custom_call_target="tpu_custom_call" | custom-call | tf_op jit(solution)/shard_map/pallas_call | solution.py:341
  11.6 0.1 collective-permute-start.2
  11.7 1.6 %collective-permute-start.4 = (f32[184,128]{1,0:T(8,128)S(1)}, f32[184,128]{1,0:T(8,128)S(1)}, u32[]{:S(2)}, u32[]{:S(2)}) collective-permute-start(f32[184,128]{1,0:T(8,128)S(1)} %get-tuple-element.17), channel_id=1, source_target_pairs={{8,0},{16,8},{24,16},{0,24},{9,1},{17,9},{25,17},{1,25},{10,2},{18... | collective-permute-start | bytes 282632 | tf_op jit(solution)/shard_map/ppermute | solution.py:353
  13.3 0.5 %collective-permute-start.3 = (f32[96,128]{1,0:T(8,128)S(1)}, f32[96,128]{1,0:T(8,128)S(1)}, u32[]{:S(2)}, u32[]{:S(2)}) collective-permute-start(f32[96,128]{1,0:T(8,128)S(1)} %get-tuple-element.21), channel_id=1, source_target_pairs={{16,0},{24,8},{0,16},{8,24},{17,1},{25,9},{1,17},{9,25},{18,2},{26... | collective-permute-start | bytes 147464 | tf_op jit(solution)/shard_map/ppermute | solution.py:353
  13.8 1.5 %collective-permute-start.5 = (f32[56,128]{1,0:T(8,128)S(1)}, f32[56,128]{1,0:T(8,128)S(1)}, u32[]{:S(2)}, u32[]{:S(2)}) collective-permute-start(f32[56,128]{1,0:T(8,128)S(1)} %get-tuple-element.24), channel_id=1, source_target_pairs={{16,0},{24,8},{0,16},{8,24},{17,1},{25,9},{1,17},{9,25},{18,2},{26... | collective-permute-start | bytes 86024 | tf_op jit(solution)/shard_map/ppermute | solution.py:353
  15.3 3.4 %collective-permute-done.5.refs_2_ = f32[56,128]{1,0:T(8,128)S(1)} collective-permute-done((f32[56,128]{1,0:T(8,128)S(1)}, f32[56,128]{1,0:T(8,128)S(1)}, u32[]{:S(2)}, u32[]{:S(2)}) %collective-permute-start.5) | collective-permute-done | bytes 28704 | tf_op jit(solution)/shard_map/ppermute | solution.py:353
  18.7 0.0 collective-permute-done.4.refs_1_
  18.7 0.7 %shard_map.31 = (f32[108,16,128]{2,1,0:T(8,128)S(1)}, f32[8,128]{1,0:T(8,128)S(1)}) custom-call(f32[12,24,128]{2,1,0:T(8,128)S(1)} %get-tuple-element.16.refs_0_, f32[184,128]{1,0:T(8,128)S(1)} %collective-permute-done.4.refs_1_, f32[56,128]{1,0:T(8,128)S(1)} %collective-permute-done.5.refs_2_), custom_call_target="tpu_custom_call" | custom-call | tf_op jit(solution)/shard_map/pallas_call | solution.py:341
  19.4 0.0 collective-permute-done.3.refs_0_
  19.4 0.1 shard_map.30
  19.5 0.0 collective-permute-done.2.refs_1_
  19.5 1.2 %shard_map.32.refs_0_ = f32[16,128]{1,0:T(8,128)S(1)} custom-call(f32[360,128]{1,0:T(8,128)S(1)} %get-tuple-element.19.refs_0_, f32[240,128]{1,0:T(8,128)S(1)} %collective-permute-done.2.refs_1_, f32[18,24,128]{2,1,0:T(8,128)S(1)} %get-tuple-element.22.refs_2_, f32[18,8,128]{2,1,0:T(8,128)S(1)} %get-tuple-element.23.refs_3_, ...), custom_call_target="tpu_custom_call" | custom-call | tf_op jit(solution)/shard_map/pallas_call | solution.py:341
  20.7 1.5 %collective-permute-start.6 = (f32[16,128]{1,0:T(8,128)S(1)}, f32[16,128]{1,0:T(8,128)S(1)}, u32[]{:S(2)}, u32[]{:S(2)}) collective-permute-start(f32[16,128]{1,0:T(8,128)S(1)} %shard_map.32.refs_0_), channel_id=1, source_target_pairs={{4,0},{0,4},{5,1},{1,5},{6,2},{2,6},{7,3},{3,7},{12,8},{8,12},{13,... | collective-permute-start | bytes 24584 | tf_op jit(solution)/shard_map/ppermute | solution.py:353
  22.2 2.2 %collective-permute-done.6.refs_1_ = f32[16,128]{1,0:T(8,128)S(1)} collective-permute-done((f32[16,128]{1,0:T(8,128)S(1)}, f32[16,128]{1,0:T(8,128)S(1)}, u32[]{:S(2)}, u32[]{:S(2)}) %collective-permute-start.6) | collective-permute-done | bytes 8224 | tf_op jit(solution)/shard_map/ppermute | solution.py:353
  24.4 0.7 %shard_map.33 = f32[6,4,4,6]{3,2,1,0:T(4,128)} custom-call(f32[16,128]{1,0:T(8,128)S(1)} %shard_map.32.refs_0_, f32[16,128]{1,0:T(8,128)S(1)} %collective-permute-done.6.refs_1_), custom_call_target="tpu_custom_call" | custom-call | tf_op jit(solution)/shard_map/pallas_call | solution.py:341
Async XLA Ops:
  1.3 10.0 %collective-permute-start = (f32[184,128]{1,0:T(8,128)S(1)}, f32[184,128]{1,0:T(8,128)S(1)}, u32[]{:S(2)}, u32[]{:S(2)}) collective-permute-start(f32[184,128]{1,0:T(8,128)S(1)} %get-tuple-element.17), channel_id=1, source_target_pairs={{1,0},{2,1},{3,2},{0,3},{5,4},{6,5},{7,6},{4,7},{9,8},{10,9},{11,1... | collective-permute-start | bytes 282632 | tf_op jit(solution)/shard_map/ppermute | solution.py:353
  6.4 4.9 %collective-permute-start.1 = (f32[72,128]{1,0:T(8,128)S(1)}, f32[72,128]{1,0:T(8,128)S(1)}, u32[]{:S(2)}, u32[]{:S(2)}) collective-permute-start(f32[72,128]{1,0:T(8,128)S(1)} %get-tuple-element.18), channel_id=1, source_target_pairs={{2,0},{3,1},{0,2},{1,3},{6,4},{7,5},{4,6},{5,7},{10,8},{11,9},{8,1... | collective-permute-start | bytes 110600 | tf_op jit(solution)/shard_map/ppermute | solution.py:353
  11.6 7.9 %collective-permute-start.2 = (f32[240,128]{1,0:T(8,128)S(1)}, f32[240,128]{1,0:T(8,128)S(1)}, u32[]{:S(2)}, u32[]{:S(2)}) collective-permute-start(f32[240,128]{1,0:T(8,128)S(1)} %get-tuple-element.20), channel_id=1, source_target_pairs={{8,0},{16,8},{24,16},{0,24},{9,1},{17,9},{25,17},{1,25},{10,2},{18... | collective-permute-start | bytes 368648 | tf_op jit(solution)/shard_map/ppermute | solution.py:353
  11.7 7.0 %collective-permute-start.4 = (f32[184,128]{1,0:T(8,128)S(1)}, f32[184,128]{1,0:T(8,128)S(1)}, u32[]{:S(2)}, u32[]{:S(2)}) collective-permute-start(f32[184,128]{1,0:T(8,128)S(1)} %get-tuple-element.17), channel_id=1, source_target_pairs={{8,0},{16,8},{24,16},{0,24},{9,1},{17,9},{25,17},{1,25},{10,2},{18... | collective-permute-start | bytes 282632 | tf_op jit(solution)/shard_map/ppermute | solution.py:353
  13.3 6.1 %collective-permute-start.3 = (f32[96,128]{1,0:T(8,128)S(1)}, f32[96,128]{1,0:T(8,128)S(1)}, u32[]{:S(2)}, u32[]{:S(2)}) collective-permute-start(f32[96,128]{1,0:T(8,128)S(1)} %get-tuple-element.21), channel_id=1, source_target_pairs={{16,0},{24,8},{0,16},{8,24},{17,1},{25,9},{1,17},{9,25},{18,2},{26... | collective-permute-start | bytes 147464 | tf_op jit(solution)/shard_map/ppermute | solution.py:353
  13.8 4.9 %collective-permute-start.5 = (f32[56,128]{1,0:T(8,128)S(1)}, f32[56,128]{1,0:T(8,128)S(1)}, u32[]{:S(2)}, u32[]{:S(2)}) collective-permute-start(f32[56,128]{1,0:T(8,128)S(1)} %get-tuple-element.24), channel_id=1, source_target_pairs={{16,0},{24,8},{0,16},{8,24},{17,1},{25,9},{1,17},{9,25},{18,2},{26... | collective-permute-start | bytes 86024 | tf_op jit(solution)/shard_map/ppermute | solution.py:353
  20.7 3.7 %collective-permute-start.6 = (f32[16,128]{1,0:T(8,128)S(1)}, f32[16,128]{1,0:T(8,128)S(1)}, u32[]{:S(2)}, u32[]{:S(2)}) collective-permute-start(f32[16,128]{1,0:T(8,128)S(1)} %shard_map.32.refs_0_), channel_id=1, source_target_pairs={{4,0},{0,4},{5,1},{1,5},{6,2},{2,6},{7,3},{3,7},{12,8},{8,12},{13,... | collective-permute-start | bytes 24584 | tf_op jit(solution)/shard_map/ppermute | solution.py:353

commit v5 on v3

--- a/solution.py
+++ b/solution.py
@@ -332,14 +332,14 @@
             out_ref[r, x] = v_ref[r, pl.ds(x, n, stride=n), :][:, :TMAX]
 
 
-def call(kernel, outs, scratch, *args, space=pltpu.VMEM):
+def call(kernel, outs, scratch, *args, space=pltpu.VMEM, fuse=False):
     return pl.pallas_call(
         kernel,
         out_shape=[jax.ShapeDtypeStruct(s, jnp.float32) for s in outs],
         in_specs=[pl.BlockSpec(memory_space=space)] * len(args),
         out_specs=[pl.BlockSpec(memory_space=pltpu.VMEM)] * len(outs),
         scratch_shapes=[pltpu.VMEM(s, jnp.float32) if isinstance(s, tuple) else s for s in scratch],
-        compiler_params=pltpu.CompilerParams(vmem_limit_bytes=8 * 2**20),
+        compiler_params=pltpu.CompilerParams(vmem_limit_bytes=8 * 2**20, allow_input_fusion=[True] * len(args) if fuse else None),
     )(*args)
 
 
@@ -360,6 +360,7 @@
         [(12, block + two, lanes)] + [(VALUES * rows, lanes) for rows in (block + two - 1, two + 1, two - 1)],
         [(18, block + 8, lanes), (12, block, lanes)],
         jnp.stack([link_x.reshape(flat), link_t.reshape(flat)]),
+        fuse=True,
     )
     near_t, far_t = ahead(near, "ta", 1), ahead(far, "ta", 2)
     near_x, edge_x = ahead(near, "gx", 1), ahead(edge, "gx", 2)

time: 25.2 us -> 25.2 us (level)
  no operation moved by 1% of the time
where the time goes in v5:
time: 25.2 us; the launch traced here: 25 us
  starting transfers between devices  10.4 us (41%)
  waiting for transfers between devices  10.4 us (41%)
  Pallas kernels  3.24 us (13%)
  other arithmetic  1 us (4%)
    ppermute x7, waiting for transfers between devices, ahead(): lax.ppermute(block, axis, [((i + distance) % count, i) for i in range(cou...  10.4 us
    ppermute x7, starting transfers between devices, ahead(): lax.ppermute(block, axis, [((i + distance) % count, i) for i in range(cou...  10.4 us
    pallas_call x5, Pallas kernels, call(): pl.pallas_call(kernel, out_shape=[jax.ShapeDtypeStruct(s, jnp.float32) fo...  3.24 us
    another operation x1, other arithmetic, local(): jnp.stack([link_x.reshape(flat), link_t.reshape(flat)])  1 us
  transfers between devices with their start and end apart: 7, of which 3 were waited for; matrix products, arithmetic and copies ran while one was open for 0% of the time, Pallas kernels for 3%

profile of v5, /device:TPU:0, one launch (start us, length us, event | category | flops | bytes accessed | tf_op | source)
XLA Modules:
  0.0 25.0 jit_solution(18137775782272240108)
XLA Ops:
  0.0 1.0 %pad_maximum_fusion.refs_0_ = f32[2,18,16,128]{3,2,1,0:T(8,128)S(1)} fusion(f32[1,18,16,128]{3,2,1,0:T(8,128)} %bitcast.3, f32[1,18,16,128]{3,2,1,0:T(8,128)} %bitcast.4), kind=kLoop, calls=%fused_computation | loop fusion | flops 73728 | bytes 589824 | tf_op jit(solution)/shard_map/stack | solution.py:362
  1.0 0.2 shard_map.28
  1.3 5.1 %collective-permute-start = (f32[184,128]{1,0:T(8,128)S(1)}, f32[184,128]{1,0:T(8,128)S(1)}, u32[]{:S(2)}, u32[]{:S(2)}) collective-permute-start(f32[184,128]{1,0:T(8,128)S(1)} %get-tuple-element.15), channel_id=1, source_target_pairs={{1,0},{2,1},{3,2},{0,3},{5,4},{6,5},{7,6},{4,7},{9,8},{10,9},{11,1... | collective-permute-start | bytes 282632 | tf_op jit(solution)/shard_map/ppermute | solution.py:348
  6.4 0.0 collective-permute-start.1
  6.4 4.9 %collective-permute-done.1.refs_2_ = f32[72,128]{1,0:T(8,128)S(1)} collective-permute-done((f32[72,128]{1,0:T(8,128)S(1)}, f32[72,128]{1,0:T(8,128)S(1)}, u32[]{:S(2)}, u32[]{:S(2)}) %collective-permute-start.1) | collective-permute-done | bytes 36896 | tf_op jit(solution)/shard_map/ppermute | solution.py:348
  11.2 0.0 collective-permute-done.refs_1_
  11.2 0.4 %shard_map.29 = (f32[360,128]{1,0:T(8,128)S(1)}, f32[240,128]{1,0:T(8,128)S(1)}, f32[96,128]{1,0:T(8,128)S(1)}) custom-call(f32[12,24,128]{2,1,0:T(8,128)S(1)} %get-tuple-element.14.refs_0_, f32[184,128]{1,0:T(8,128)S(1)} %collective-permute-done.refs_1_, f32[72,128]{1,0:T(8,128)S(1)} %collective-permute-done.1.refs_2_), custom_call_target="tpu_custom_call" | custom-call | tf_op jit(solution)/shard_map/pallas_call | solution.py:336
  11.6 0.1 collective-permute-start.2
  11.7 1.6 %collective-permute-start.4 = (f32[184,128]{1,0:T(8,128)S(1)}, f32[184,128]{1,0:T(8,128)S(1)}, u32[]{:S(2)}, u32[]{:S(2)}) collective-permute-start(f32[184,128]{1,0:T(8,128)S(1)} %get-tuple-element.15), channel_id=1, source_target_pairs={{8,0},{16,8},{24,16},{0,24},{9,1},{17,9},{25,17},{1,25},{10,2},{18... | collective-permute-start | bytes 282632 | tf_op jit(solution)/shard_map/ppermute | solution.py:348
  13.3 0.5 %collective-permute-start.3 = (f32[96,128]{1,0:T(8,128)S(1)}, f32[96,128]{1,0:T(8,128)S(1)}, u32[]{:S(2)}, u32[]{:S(2)}) collective-permute-start(f32[96,128]{1,0:T(8,128)S(1)} %get-tuple-element.19), channel_id=1, source_target_pairs={{16,0},{24,8},{0,16},{8,24},{17,1},{25,9},{1,17},{9,25},{18,2},{26... | collective-permute-start | bytes 147464 | tf_op jit(solution)/shard_map/ppermute | solution.py:348
  13.8 1.5 %collective-permute-start.5 = (f32[56,128]{1,0:T(8,128)S(1)}, f32[56,128]{1,0:T(8,128)S(1)}, u32[]{:S(2)}, u32[]{:S(2)}) collective-permute-start(f32[56,128]{1,0:T(8,128)S(1)} %get-tuple-element.20), channel_id=1, source_target_pairs={{16,0},{24,8},{0,16},{8,24},{17,1},{25,9},{1,17},{9,25},{18,2},{26... | collective-permute-start | bytes 86024 | tf_op jit(solution)/shard_map/ppermute | solution.py:348
  15.3 3.4 %collective-permute-done.5.refs_2_ = f32[56,128]{1,0:T(8,128)S(1)} collective-permute-done((f32[56,128]{1,0:T(8,128)S(1)}, f32[56,128]{1,0:T(8,128)S(1)}, u32[]{:S(2)}, u32[]{:S(2)}) %collective-permute-start.5) | collective-permute-done | bytes 28704 | tf_op jit(solution)/shard_map/ppermute | solution.py:348
  18.7 0.0 collective-permute-done.4.refs_1_
  18.7 0.7 %shard_map.30 = (f32[108,16,128]{2,1,0:T(8,128)S(1)}, f32[8,128]{1,0:T(8,128)S(1)}) custom-call(f32[12,24,128]{2,1,0:T(8,128)S(1)} %get-tuple-element.14.refs_0_, f32[184,128]{1,0:T(8,128)S(1)} %collective-permute-done.4.refs_1_, f32[56,128]{1,0:T(8,128)S(1)} %collective-permute-done.5.refs_2_), custom_call_target="tpu_custom_call" | custom-call | tf_op jit(solution)/shard_map/pallas_call | solution.py:336
  19.4 0.0 collective-permute-done.3.refs_2_
  19.4 0.0 collective-permute-done.2.refs_1_
  19.4 1.2 %shard_map.31.refs_0_ = f32[16,128]{1,0:T(8,128)S(1)} custom-call(f32[360,128]{1,0:T(8,128)S(1)} %get-tuple-element.17.refs_0_, f32[240,128]{1,0:T(8,128)S(1)} %collective-permute-done.2.refs_1_, f32[96,128]{1,0:T(8,128)S(1)} %collective-permute-done.3.refs_2_, f32[108,16,128]{2,1,0:T(8,128)S(1)} %get-tuple-element.21.refs_3_, ...), custom_call_target="tpu_custom_call" | custom-call | tf_op jit(solution)/shard_map/pallas_call | solution.py:336
  20.6 1.5 %collective-permute-start.6 = (f32[16,128]{1,0:T(8,128)S(1)}, f32[16,128]{1,0:T(8,128)S(1)}, u32[]{:S(2)}, u32[]{:S(2)}) collective-permute-start(f32[16,128]{1,0:T(8,128)S(1)} %shard_map.31.refs_0_), channel_id=1, source_target_pairs={{4,0},{0,4},{5,1},{1,5},{6,2},{2,6},{7,3},{3,7},{12,8},{8,12},{13,... | collective-permute-start | bytes 24584 | tf_op jit(solution)/shard_map/ppermute | solution.py:348
  22.2 2.2 %collective-permute-done.6.refs_1_ = f32[16,128]{1,0:T(8,128)S(1)} collective-permute-done((f32[16,128]{1,0:T(8,128)S(1)}, f32[16,128]{1,0:T(8,128)S(1)}, u32[]{:S(2)}, u32[]{:S(2)}) %collective-permute-start.6) | collective-permute-done | bytes 8224 | tf_op jit(solution)/shard_map/ppermute | solution.py:348
  24.3 0.7 %shard_map.32 = f32[6,4,4,6]{3,2,1,0:T(4,128)} custom-call(f32[16,128]{1,0:T(8,128)S(1)} %shard_map.31.refs_0_, f32[16,128]{1,0:T(8,128)S(1)} %collective-permute-done.6.refs_1_), custom_call_target="tpu_custom_call" | custom-call | tf_op jit(solution)/shard_map/pallas_call | solution.py:336
Async XLA Ops:
  1.3 10.0 %collective-permute-start = (f32[184,128]{1,0:T(8,128)S(1)}, f32[184,128]{1,0:T(8,128)S(1)}, u32[]{:S(2)}, u32[]{:S(2)}) collective-permute-start(f32[184,128]{1,0:T(8,128)S(1)} %get-tuple-element.15), channel_id=1, source_target_pairs={{1,0},{2,1},{3,2},{0,3},{5,4},{6,5},{7,6},{4,7},{9,8},{10,9},{11,1... | collective-permute-start | bytes 282632 | tf_op jit(solution)/shard_map/ppermute | solution.py:348
  6.4 4.9 %collective-permute-start.1 = (f32[72,128]{1,0:T(8,128)S(1)}, f32[72,128]{1,0:T(8,128)S(1)}, u32[]{:S(2)}, u32[]{:S(2)}) collective-permute-start(f32[72,128]{1,0:T(8,128)S(1)} %get-tuple-element.16), channel_id=1, source_target_pairs={{2,0},{3,1},{0,2},{1,3},{6,4},{7,5},{4,6},{5,7},{10,8},{11,9},{8,1... | collective-permute-start | bytes 110600 | tf_op jit(solution)/shard_map/ppermute | solution.py:348
  11.6 7.8 %collective-permute-start.2 = (f32[240,128]{1,0:T(8,128)S(1)}, f32[240,128]{1,0:T(8,128)S(1)}, u32[]{:S(2)}, u32[]{:S(2)}) collective-permute-start(f32[240,128]{1,0:T(8,128)S(1)} %get-tuple-element.18), channel_id=1, source_target_pairs={{8,0},{16,8},{24,16},{0,24},{9,1},{17,9},{25,17},{1,25},{10,2},{18... | collective-permute-start | bytes 368648 | tf_op jit(solution)/shard_map/ppermute | solution.py:348
  11.7 7.0 %collective-permute-start.4 = (f32[184,128]{1,0:T(8,128)S(1)}, f32[184,128]{1,0:T(8,128)S(1)}, u32[]{:S(2)}, u32[]{:S(2)}) collective-permute-start(f32[184,128]{1,0:T(8,128)S(1)} %get-tuple-element.15), channel_id=1, source_target_pairs={{8,0},{16,8},{24,16},{0,24},{9,1},{17,9},{25,17},{1,25},{10,2},{18... | collective-permute-start | bytes 282632 | tf_op jit(solution)/shard_map/ppermute | solution.py:348
  13.3 6.1 %collective-permute-start.3 = (f32[96,128]{1,0:T(8,128)S(1)}, f32[96,128]{1,0:T(8,128)S(1)}, u32[]{:S(2)}, u32[]{:S(2)}) collective-permute-start(f32[96,128]{1,0:T(8,128)S(1)} %get-tuple-element.19), channel_id=1, source_target_pairs={{16,0},{24,8},{0,16},{8,24},{17,1},{25,9},{1,17},{9,25},{18,2},{26... | collective-permute-start | bytes 147464 | tf_op jit(solution)/shard_map/ppermute | solution.py:348
  13.8 4.9 %collective-permute-start.5 = (f32[56,128]{1,0:T(8,128)S(1)}, f32[56,128]{1,0:T(8,128)S(1)}, u32[]{:S(2)}, u32[]{:S(2)}) collective-permute-start(f32[56,128]{1,0:T(8,128)S(1)} %get-tuple-element.20), channel_id=1, source_target_pairs={{16,0},{24,8},{0,16},{8,24},{17,1},{25,9},{1,17},{9,25},{18,2},{26... | collective-permute-start | bytes 86024 | tf_op jit(solution)/shard_map/ppermute | solution.py:348
  20.6 3.7 %collective-permute-start.6 = (f32[16,128]{1,0:T(8,128)S(1)}, f32[16,128]{1,0:T(8,128)S(1)}, u32[]{:S(2)}, u32[]{:S(2)}) collective-permute-start(f32[16,128]{1,0:T(8,128)S(1)} %shard_map.31.refs_0_), channel_id=1, source_target_pairs={{4,0},{0,4},{5,1},{1,5},{6,2},{2,6},{7,3},{3,7},{12,8},{8,12},{13,... | collective-permute-start | bytes 24584 | tf_op jit(solution)/shard_map/ppermute | solution.py:348

commit v6 on v4

--- a/solution.py
+++ b/solution.py
@@ -337,14 +337,14 @@
             out_ref[r, x] = v_ref[r, pl.ds(x, n, stride=n), :][:, :TMAX]
 
 
-def call(kernel, outs, scratch, *args, space=pltpu.VMEM):
+def call(kernel, outs, scratch, *args, space=pltpu.VMEM, fuse=False):
     return pl.pallas_call(
         kernel,
         out_shape=[jax.ShapeDtypeStruct(s, jnp.float32) for s in outs],
         in_specs=[pl.BlockSpec(memory_space=space)] * len(args),
         out_specs=[pl.BlockSpec(memory_space=pltpu.VMEM)] * len(outs),
         scratch_shapes=[pltpu.VMEM(s, jnp.float32) if isinstance(s, tuple) else s for s in scratch],
-        compiler_params=pltpu.CompilerParams(vmem_limit_bytes=8 * 2**20),
+        compiler_params=pltpu.CompilerParams(vmem_limit_bytes=8 * 2**20, allow_input_fusion=[True] * len(args) if fuse else None),
     )(*args)
 
 
@@ -365,6 +365,7 @@
         [(12, block + two, lanes)] + [(VALUES * rows, lanes) for rows in (block + two - 1, two + 1, two - 1)],
         [(18, block + 8, lanes), (12, block, lanes)],
         jnp.stack([link_x.reshape(flat), link_t.reshape(flat)]),
+        fuse=True,
     )
     near_t, far_t = ahead(near, "ta", 1), ahead(far, "ta", 2)
     near_x, edge_x = ahead(near, "gx", 1), ahead(edge, "gx", 2)

time: 25.2 us -> 25.2 us (level)
  no operation moved by 1% of the time
where the time goes in v6:
time: 25.2 us; the launch traced here: 25.1 us
  starting transfers between devices  10.4 us (41%)
  waiting for transfers between devices  10.4 us (41%)
  Pallas kernels  3.26 us (13%)
  other arithmetic  1 us (4%)
    ppermute x7, waiting for transfers between devices, ahead(): lax.ppermute(block, axis, [((i + distance) % count, i) for i in range(cou...  10.4 us
    ppermute x7, starting transfers between devices, ahead(): lax.ppermute(block, axis, [((i + distance) % count, i) for i in range(cou...  10.4 us
    pallas_call x6, Pallas kernels, call(): pl.pallas_call(kernel, out_shape=[jax.ShapeDtypeStruct(s, jnp.float32) fo...  3.26 us
    another operation x1, other arithmetic, local(): jnp.stack([link_x.reshape(flat), link_t.reshape(flat)])  1 us
  transfers between devices with their start and end apart: 7, of which 3 were waited for; matrix products, arithmetic and copies ran while one was open for 0% of the time, Pallas kernels for 3%

profile of v6, /device:TPU:0, one launch (start us, length us, event | category | flops | bytes accessed | tf_op | source)
XLA Modules:
  0.0 25.1 jit_solution(4030272121425822088)
XLA Ops:
  0.0 1.0 %pad_maximum_fusion.refs_0_ = f32[2,18,16,128]{3,2,1,0:T(8,128)S(1)} fusion(f32[1,18,16,128]{3,2,1,0:T(8,128)} %bitcast.3, f32[1,18,16,128]{3,2,1,0:T(8,128)} %bitcast.4), kind=kLoop, calls=%fused_computation | loop fusion | flops 73728 | bytes 589824 | tf_op jit(solution)/shard_map/stack | solution.py:367
  1.0 0.2 shard_map.28
  1.3 5.1 %collective-permute-start = (f32[184,128]{1,0:T(8,128)S(1)}, f32[184,128]{1,0:T(8,128)S(1)}, u32[]{:S(2)}, u32[]{:S(2)}) collective-permute-start(f32[184,128]{1,0:T(8,128)S(1)} %get-tuple-element.17), channel_id=1, source_target_pairs={{1,0},{2,1},{3,2},{0,3},{5,4},{6,5},{7,6},{4,7},{9,8},{10,9},{11,1... | collective-permute-start | bytes 282632 | tf_op jit(solution)/shard_map/ppermute | solution.py:353
  6.4 0.0 collective-permute-start.1
  6.4 4.9 %collective-permute-done.1.refs_2_ = f32[72,128]{1,0:T(8,128)S(1)} collective-permute-done((f32[72,128]{1,0:T(8,128)S(1)}, f32[72,128]{1,0:T(8,128)S(1)}, u32[]{:S(2)}, u32[]{:S(2)}) %collective-permute-start.1) | collective-permute-done | bytes 36896 | tf_op jit(solution)/shard_map/ppermute | solution.py:353
  11.2 0.0 collective-permute-done.refs_1_
  11.2 0.4 %shard_map.29 = (f32[360,128]{1,0:T(8,128)S(1)}, f32[240,128]{1,0:T(8,128)S(1)}, f32[96,128]{1,0:T(8,128)S(1)}) custom-call(f32[12,24,128]{2,1,0:T(8,128)S(1)} %get-tuple-element.16.refs_0_, f32[184,128]{1,0:T(8,128)S(1)} %collective-permute-done.refs_1_, f32[72,128]{1,0:T(8,128)S(1)} %collective-permute-done.1.refs_2_), custom_call_target="tpu_custom_call" | custom-call | tf_op jit(solution)/shard_map/pallas_call | solution.py:341
  11.6 0.1 collective-permute-start.2
  11.7 1.6 %collective-permute-start.4 = (f32[184,128]{1,0:T(8,128)S(1)}, f32[184,128]{1,0:T(8,128)S(1)}, u32[]{:S(2)}, u32[]{:S(2)}) collective-permute-start(f32[184,128]{1,0:T(8,128)S(1)} %get-tuple-element.17), channel_id=1, source_target_pairs={{8,0},{16,8},{24,16},{0,24},{9,1},{17,9},{25,17},{1,25},{10,2},{18... | collective-permute-start | bytes 282632 | tf_op jit(solution)/shard_map/ppermute | solution.py:353
  13.3 0.5 %collective-permute-start.3 = (f32[96,128]{1,0:T(8,128)S(1)}, f32[96,128]{1,0:T(8,128)S(1)}, u32[]{:S(2)}, u32[]{:S(2)}) collective-permute-start(f32[96,128]{1,0:T(8,128)S(1)} %get-tuple-element.21), channel_id=1, source_target_pairs={{16,0},{24,8},{0,16},{8,24},{17,1},{25,9},{1,17},{9,25},{18,2},{26... | collective-permute-start | bytes 147464 | tf_op jit(solution)/shard_map/ppermute | solution.py:353
  13.8 1.5 %collective-permute-start.5 = (f32[56,128]{1,0:T(8,128)S(1)}, f32[56,128]{1,0:T(8,128)S(1)}, u32[]{:S(2)}, u32[]{:S(2)}) collective-permute-start(f32[56,128]{1,0:T(8,128)S(1)} %get-tuple-element.24), channel_id=1, source_target_pairs={{16,0},{24,8},{0,16},{8,24},{17,1},{25,9},{1,17},{9,25},{18,2},{26... | collective-permute-start | bytes 86024 | tf_op jit(solution)/shard_map/ppermute | solution.py:353
  15.3 3.4 %collective-permute-done.5.refs_2_ = f32[56,128]{1,0:T(8,128)S(1)} collective-permute-done((f32[56,128]{1,0:T(8,128)S(1)}, f32[56,128]{1,0:T(8,128)S(1)}, u32[]{:S(2)}, u32[]{:S(2)}) %collective-permute-start.5) | collective-permute-done | bytes 28704 | tf_op jit(solution)/shard_map/ppermute | solution.py:353
  18.7 0.0 collective-permute-done.4.refs_1_
  18.7 0.7 %shard_map.31 = (f32[108,16,128]{2,1,0:T(8,128)S(1)}, f32[8,128]{1,0:T(8,128)S(1)}) custom-call(f32[12,24,128]{2,1,0:T(8,128)S(1)} %get-tuple-element.16.refs_0_, f32[184,128]{1,0:T(8,128)S(1)} %collective-permute-done.4.refs_1_, f32[56,128]{1,0:T(8,128)S(1)} %collective-permute-done.5.refs_2_), custom_call_target="tpu_custom_call" | custom-call | tf_op jit(solution)/shard_map/pallas_call | solution.py:341
  19.4 0.0 collective-permute-done.3.refs_0_
  19.4 0.1 shard_map.30
  19.5 0.0 collective-permute-done.2.refs_1_
  19.5 1.2 %shard_map.32.refs_0_ = f32[16,128]{1,0:T(8,128)S(1)} custom-call(f32[360,128]{1,0:T(8,128)S(1)} %get-tuple-element.19.refs_0_, f32[240,128]{1,0:T(8,128)S(1)} %collective-permute-done.2.refs_1_, f32[18,24,128]{2,1,0:T(8,128)S(1)} %get-tuple-element.22.refs_2_, f32[18,8,128]{2,1,0:T(8,128)S(1)} %get-tuple-element.23.refs_3_, ...), custom_call_target="tpu_custom_call" | custom-call | tf_op jit(solution)/shard_map/pallas_call | solution.py:341
  20.7 1.5 %collective-permute-start.6 = (f32[16,128]{1,0:T(8,128)S(1)}, f32[16,128]{1,0:T(8,128)S(1)}, u32[]{:S(2)}, u32[]{:S(2)}) collective-permute-start(f32[16,128]{1,0:T(8,128)S(1)} %shard_map.32.refs_0_), channel_id=1, source_target_pairs={{4,0},{0,4},{5,1},{1,5},{6,2},{2,6},{7,3},{3,7},{12,8},{8,12},{13,... | collective-permute-start | bytes 24584 | tf_op jit(solution)/shard_map/ppermute | solution.py:353
  22.2 2.2 %collective-permute-done.6.refs_1_ = f32[16,128]{1,0:T(8,128)S(1)} collective-permute-done((f32[16,128]{1,0:T(8,128)S(1)}, f32[16,128]{1,0:T(8,128)S(1)}, u32[]{:S(2)}, u32[]{:S(2)}) %collective-permute-start.6) | collective-permute-done | bytes 8224 | tf_op jit(solution)/shard_map/ppermute | solution.py:353
  24.4 0.7 %shard_map.33 = f32[6,4,4,6]{3,2,1,0:T(4,128)} custom-call(f32[16,128]{1,0:T(8,128)S(1)} %shard_map.32.refs_0_, f32[16,128]{1,0:T(8,128)S(1)} %collective-permute-done.6.refs_1_), custom_call_target="tpu_custom_call" | custom-call | tf_op jit(solution)/shard_map/pallas_call | solution.py:341
Async XLA Ops:
  1.3 10.0 %collective-permute-start = (f32[184,128]{1,0:T(8,128)S(1)}, f32[184,128]{1,0:T(8,128)S(1)}, u32[]{:S(2)}, u32[]{:S(2)}) collective-permute-start(f32[184,128]{1,0:T(8,128)S(1)} %get-tuple-element.17), channel_id=1, source_target_pairs={{1,0},{2,1},{3,2},{0,3},{5,4},{6,5},{7,6},{4,7},{9,8},{10,9},{11,1... | collective-permute-start | bytes 282632 | tf_op jit(solution)/shard_map/ppermute | solution.py:353
  6.4 4.9 %collective-permute-start.1 = (f32[72,128]{1,0:T(8,128)S(1)}, f32[72,128]{1,0:T(8,128)S(1)}, u32[]{:S(2)}, u32[]{:S(2)}) collective-permute-start(f32[72,128]{1,0:T(8,128)S(1)} %get-tuple-element.18), channel_id=1, source_target_pairs={{2,0},{3,1},{0,2},{1,3},{6,4},{7,5},{4,6},{5,7},{10,8},{11,9},{8,1... | collective-permute-start | bytes 110600 | tf_op jit(solution)/shard_map/ppermute | solution.py:353
  11.6 7.9 %collective-permute-start.2 = (f32[240,128]{1,0:T(8,128)S(1)}, f32[240,128]{1,0:T(8,128)S(1)}, u32[]{:S(2)}, u32[]{:S(2)}) collective-permute-start(f32[240,128]{1,0:T(8,128)S(1)} %get-tuple-element.20), channel_id=1, source_target_pairs={{8,0},{16,8},{24,16},{0,24},{9,1},{17,9},{25,17},{1,25},{10,2},{18... | collective-permute-start | bytes 368648 | tf_op jit(solution)/shard_map/ppermute | solution.py:353
  11.7 7.0 %collective-permute-start.4 = (f32[184,128]{1,0:T(8,128)S(1)}, f32[184,128]{1,0:T(8,128)S(1)}, u32[]{:S(2)}, u32[]{:S(2)}) collective-permute-start(f32[184,128]{1,0:T(8,128)S(1)} %get-tuple-element.17), channel_id=1, source_target_pairs={{8,0},{16,8},{24,16},{0,24},{9,1},{17,9},{25,17},{1,25},{10,2},{18... | collective-permute-start | bytes 282632 | tf_op jit(solution)/shard_map/ppermute | solution.py:353
  13.3 6.1 %collective-permute-start.3 = (f32[96,128]{1,0:T(8,128)S(1)}, f32[96,128]{1,0:T(8,128)S(1)}, u32[]{:S(2)}, u32[]{:S(2)}) collective-permute-start(f32[96,128]{1,0:T(8,128)S(1)} %get-tuple-element.21), channel_id=1, source_target_pairs={{16,0},{24,8},{0,16},{8,24},{17,1},{25,9},{1,17},{9,25},{18,2},{26... | collective-permute-start | bytes 147464 | tf_op jit(solution)/shard_map/ppermute | solution.py:353
  13.8 4.9 %collective-permute-start.5 = (f32[56,128]{1,0:T(8,128)S(1)}, f32[56,128]{1,0:T(8,128)S(1)}, u32[]{:S(2)}, u32[]{:S(2)}) collective-permute-start(f32[56,128]{1,0:T(8,128)S(1)} %get-tuple-element.24), channel_id=1, source_target_pairs={{16,0},{24,8},{0,16},{8,24},{17,1},{25,9},{1,17},{9,25},{18,2},{26... | collective-permute-start | bytes 86024 | tf_op jit(solution)/shard_map/ppermute | solution.py:353
  20.7 3.7 %collective-permute-start.6 = (f32[16,128]{1,0:T(8,128)S(1)}, f32[16,128]{1,0:T(8,128)S(1)}, u32[]{:S(2)}, u32[]{:S(2)}) collective-permute-start(f32[16,128]{1,0:T(8,128)S(1)} %shard_map.32.refs_0_), channel_id=1, source_target_pairs={{4,0},{0,4},{5,1},{1,5},{6,2},{2,6},{7,3},{3,7},{12,8},{8,12},{13,... | collective-permute-start | bytes 24584 | tf_op jit(solution)/shard_map/ppermute | solution.py:353
